TPU v7x, 32 devices: a whole 2x2x4 slice. The times are simulated.
32 devices in a mesh: section: 4 (over z), tensor: 4 (over y, x), dp: 2 (over core).
Axes of the slice: x: 2, y: 2, z: 4, core: 2. Of those that a mesh axis runs over, the one named last changes fastest.
Arguments:
- forward_rows: bfloat16 [4, 2, 192, 8192], P('section', 'dp', None, 'tensor'), may hold values from -6 to 6
- saved_rows: bfloat16 [4, 2, 192, 8192], P('section', 'dp', None, 'tensor'), may hold values from -40.5 to 40.5
- output_grad: bfloat16 [4, 2, 192, 8192], P('section', 'dp', None, 'tensor'), may hold values from -1.27 to 1.27
- lengths: int32 [4, 2, 2], P('section', 'dp'), may hold values from 1 to 96
- norm_gain: bfloat16 [4, 8192], P('section', 'tensor'), may hold values from 0.5 to 1.5
- down_map: bfloat16 [4, 192, 8192], P('section', None, 'tensor'), may hold values from -0.067396115 to 0.067396115
- up_map: bfloat16 [4, 192, 8192], P('section', None, 'tensor'), may hold values from -1.0625 to 1.0625
Outputs:
- next_inputs: bfloat16 [4, 2, 192, 8192], P('section', 'dp', None, 'tensor')
- next_grads: bfloat16 [4, 2, 192, 8192], P('section', 'dp', None, 'tensor')
- grad_down: bfloat16 [4, 192, 8192], P('section', 'dp', 'tensor')
- grad_up: bfloat16 [4, 192, 8192], P('section', 'dp', 'tensor')
All inputs are finite; a program needn't handle non-finite values.
Results may differ from a plain program's by a relative error of at most 0.02.
Values may be sent and summed in bfloat16 or wider, within the bound.
No kernel may reach another device: no remote copies, remote signals or barrier semaphores. Data moves between devices by JAX's collectives and lax.ppermute only.
A program may use at most 64 MiB of HBM per device.

v0:
```python
import jax
import jax.numpy as jnp
from jax import lax
from jax.sharding import PartitionSpec as P

EPSILON = 1e-05


def padded_2(cells, sides, width):
    for axis, dim in sides:
        count = lax.axis_size(axis)
        ends = count - 1
        head = lax.slice_in_dim(cells, 0, width, axis=dim)
        tail = lax.slice_in_dim(cells, cells.shape[dim] - width, cells.shape[dim], axis=dim)
        cells = jnp.concatenate(
            [
                lax.ppermute(tail, axis, [(i, (i + 1) % count) for i in range(ends)]),
                cells,
                lax.ppermute(head, axis, [((i + 1) % count, i) for i in range(ends)]),
            ],
            axis=dim,
        )
    return cells


def contract_last(left_side, right_side):
    return lax.dot_general(
        left_side, right_side, (((1,), (1,)), ((), ())), preferred_element_type=jnp.float32
    )


def contract_rows(left_side, right_side):
    return lax.dot_general(
        left_side, right_side, (((0,), (0,)), ((), ())), preferred_element_type=jnp.float32
    )


def silu_slope(values):
    gate_value = jax.nn.sigmoid(values)
    return gate_value * (1.0 + values * (1.0 - gate_value))


def shards(forward_rows, saved_rows, output_grad, lengths, norm_gain, down_map, up_map):
    forward_block = forward_rows[0, 0]
    saved_block = saved_rows[0, 0]
    incoming = output_grad[0, 0]
    seq_lengths = lengths[0, 0]
    gain_cols = norm_gain[0].astype(jnp.float32)
    down_cols = down_map[0]
    up_cols = up_map[0]
    row_count = forward_block.shape[0]
    seq_rows = row_count // 2
    full_width = forward_block.shape[1] * lax.axis_size("tensor")
    forward_values = forward_block.astype(jnp.float32)
    saved_values = saved_block.astype(jnp.float32)
    forward_total, saved_total = lax.psum(
        (
            jnp.sum(forward_values * forward_values, axis=1),
            jnp.sum(saved_values * saved_values, axis=1),
        ),
        "tensor",
    )
    forward_scale = lax.rsqrt(forward_total / full_width + EPSILON)[:, None]
    saved_scale = lax.rsqrt(saved_total / full_width + EPSILON)[:, None]
    forward_normed = (forward_values * forward_scale * gain_cols).astype(jnp.bfloat16)
    saved_normed = (saved_values * saved_scale * gain_cols).astype(jnp.bfloat16)
    position = jnp.arange(row_count, dtype=jnp.int32)
    length_limit = jnp.where(position // seq_rows == 0, seq_lengths[0], seq_lengths[1])
    keep_rows = position % seq_rows < length_limit
    kept_grad = jnp.where(keep_rows[:, None], incoming, jnp.zeros_like(incoming))
    forward_part = contract_last(forward_normed, down_cols)
    saved_part = contract_last(saved_normed, down_cols)
    slope_part = contract_last(kept_grad, up_cols)
    forward_share, saved_share, slope_share = (
        lax.psum_scatter(
            forward_part.astype(jnp.bfloat16), "tensor", scatter_dimension=1, tiled=True
        ).astype(jnp.float32),
        lax.psum_scatter(
            saved_part.astype(jnp.bfloat16), "tensor", scatter_dimension=1, tiled=True
        ).astype(jnp.float32),
        lax.psum_scatter(
            slope_part.astype(jnp.bfloat16), "tensor", scatter_dimension=1, tiled=True
        ).astype(jnp.float32),
    )
    forward_act, saved_act, back_rank = (
        lax.all_gather(
            jax.nn.silu(forward_share).astype(jnp.bfloat16), "tensor", axis=1, tiled=True
        ),
        lax.all_gather(jax.nn.silu(saved_share).astype(jnp.bfloat16), "tensor", axis=1, tiled=True),
        lax.all_gather(
            (slope_share * silu_slope(saved_share)).astype(jnp.bfloat16),
            "tensor",
            axis=1,
            tiled=True,
        ),
    )
    forward_out = (
        forward_values + jnp.dot(forward_act, up_cols, preferred_element_type=jnp.float32)
    ).astype(jnp.bfloat16)
    back_normed = jnp.dot(back_rank, down_cols, preferred_element_type=jnp.float32)
    weighted = gain_cols * back_normed
    correction = lax.psum(jnp.sum(saved_values * weighted, axis=1), "tensor")[:, None] / full_width
    scale_cube = saved_scale * saved_scale * saved_scale
    grad_rows = (
        kept_grad.astype(jnp.float32)
        + saved_scale * weighted
        - saved_values * scale_cube * correction
    ).astype(jnp.bfloat16)
    section_edges = jnp.stack([grad_rows, forward_out], axis=0)
    padded = padded_2(section_edges, (("section", 0),), 1)
    down_part = contract_rows(back_rank, saved_normed)
    up_part = contract_rows(saved_act, kept_grad)
    down_sum, up_sum = (
        lax.psum_scatter(
            down_part.astype(jnp.bfloat16), "dp", scatter_dimension=0, tiled=True
        ).astype(jnp.float32),
        lax.psum_scatter(
            up_part.astype(jnp.bfloat16), "dp", scatter_dimension=0, tiled=True
        ).astype(jnp.float32),
    )
    mean_weight = 1.0 / lax.axis_size("dp")
    grad_down = (down_sum * mean_weight).astype(jnp.bfloat16)
    grad_up = (up_sum * mean_weight).astype(jnp.bfloat16)
    return (padded[0][None, None], padded[3][None, None], grad_down[None], grad_up[None])


def solution(mesh):
    placed = (
        P("section", "dp", None, "tensor"),
        P("section", "dp", None, "tensor"),
        P("section", "dp", None, "tensor"),
        P("section", "dp", None),
        P("section", "tensor"),
        P("section", None, "tensor"),
        P("section", None, "tensor"),
    )
    return jax.shard_map(
        shards,
        mesh=mesh,
        in_specs=placed,
        out_specs=(
            P("section", "dp", None, "tensor"),
            P("section", "dp", None, "tensor"),
            P("section", "dp", "tensor"),
            P("section", "dp", "tensor"),
        ),
        check_vma=False,
    )
```

profile of v0, /device:TPU:0, one launch (start us, length us, event | category | flops | bytes accessed | tf_op | source)
XLA Modules:
  0.0 157.6 jit_solution(3007640196093150440)
XLA Ops:
  7.2 0.0 copy-start
  7.2 0.0 reduce-scatter.10.cloned.1.call-start
  7.2 0.8 mul.144
  8.0 0.0 copy-start.7
  8.0 0.0 copy-start.4
  8.0 1.4 fusion.10
  9.5 11.4 %psum.22 = f32[192]{0:T(256)S(1)} all-reduce(f32[192]{0:T(256)S(1)} %fusion.10), channel_id=1, replica_groups=mesh['section'=4,'tensor'=4,'dp'=2] {'tensor'}, use_global_device_ids=true, to_apply=%region_4.5 | all-reduce | flops 192 | bytes 1536 | tf_op jit(solution)/shard_map/psum | solution.py:56
  20.9 0.0 copy-done
  20.9 2.2 %convolution_convert_fusion.2 = bf16[192,192]{0,1:T(8,128)(2,1)} fusion(bf16[1,1,192,2048]{3,2,1,0:T(8,128)(2,1)} %param.8, bf16[1,192,2048]{2,1,0:T(8,128)(2,1)S(1)} %copy-done, f32[192]{0:T(256)S(1)} %get-tuple-element.9, f32[2048]{0:T(1024)S(1)} %bitcast.82), kind=kOutput, calls=%fused_computation.27 | convolution fusion | flops 152604672 | bytes 1655552 | tf_op jit(solution)/shard_map/dot_general | solution.py:27
  23.1 0.0 copy-start.2
  23.1 0.0 reduce-scatter.10.cloned.1.call-update
  23.1 0.0 reduce-scatter.8.cloned.1.call-start
  23.2 0.0 copy-done.7
  23.2 0.6 fusion.57
  23.8 1.3 fusion.54
  25.1 0.0 copy-done.4
  25.1 0.0 copy-start.1
  25.1 2.3 %convolution_convert_fusion.3 = bf16[192,192]{0,1:T(8,128)(2,1)} fusion(bf16[1,192,2048]{2,1,0:T(8,128)(2,1)} %param.13, bf16[1,1,192,2048]{3,2,1,0:T(8,128)(2,1)S(1)} %copy-done.4, pred[192]{0:T(512)(128)(4,1)S(1)} %fusion.54), kind=kOutput, calls=%fused_computation.28 | convolution fusion | flops 151425024 | bytes 1646784 | tf_op jit(solution)/shard_map/dot_general | solution.py:27
  27.4 0.0 reduce-scatter.8.cloned.1.call-update
  27.5 0.0 reduce-scatter.6.cloned.1.call-start
  27.5 0.0 copy-done.2
  27.5 0.2 fusion.7
  27.8 19.0 %reduce-scatter.10.cloned.1.call-done = bf16[192,48]{0,1:T(8,128)(2,1)} async-done(((bf16[192,192]{0,1:T(8,128)(2,1)}), bf16[192,48]{0,1:T(8,128)(2,1)}) %reduce-scatter.10.cloned.1.call-update) | async-done | bytes 18448 | tf_op jit(solution)/shard_map/reduce_scatter | solution.py:78
  46.8 27.5 %reduce-scatter.8.cloned.1.call-done = bf16[192,48]{0,1:T(8,128)(2,1)} async-done(((bf16[192,192]{0,1:T(8,128)(2,1)}), bf16[192,48]{0,1:T(8,128)(2,1)}) %reduce-scatter.8.cloned.1.call-update) | async-done | bytes 18448 | tf_op jit(solution)/shard_map/reduce_scatter | solution.py:81
  74.3 0.8 fusion.53
  75.1 8.3 %all_gather.10 = bf16[192,192]{0,1:T(8,128)(2,1)S(1)} all-gather(bf16[192,48]{0,1:T(8,128)(2,1)S(1)} %get-tuple-element.7), channel_id=1, replica_groups=mesh['section'=4,'tensor'=4,'dp'=2] {'tensor'}, dimensions={1}, use_global_device_ids=true | all-gather | bytes 92160 | tf_op jit(solution)/shard_map/all_gather | solution.py:90
  83.4 0.0 copy-done.1
  83.4 0.5 fusion.14
  83.9 8.9 %all-reduce = (f32[192]{0:T(256)S(1)}, f32[192]{0:T(256)S(1)}) all-reduce(f32[192]{0:T(256)S(1)} %fusion.7, f32[192]{0:T(256)S(1)} %get-tuple-element.12), channel_id=1, replica_groups=mesh['section'=4,'tensor'=4,'dp'=2] {'tensor'}, use_global_device_ids=true, to_apply=%region_1.0 | all-reduce | flops 384 | bytes 3072 | tf_op jit(solution)/shard_map/psum | solution.py:56
  92.8 2.2 %convolution_convert_fusion.4 = bf16[192,192]{0,1:T(8,128)(2,1)} fusion(bf16[1,1,192,2048]{3,2,1,0:T(8,128)(2,1)} %param.7, bf16[1,192,2048]{2,1,0:T(8,128)(2,1)S(1)} %copy-done, f32[2048]{0:T(1024)S(1)} %bitcast.84, f32[192]{0:T(256)S(1)} %add_rsqrt_fusion.1), kind=kOutput, calls=%fused_computation.29 | convolution fusion | flops 152604672 | bytes 1655552 | tf_op jit(solution)/shard_map/dot_general | solution.py:27
  95.0 0.0 reduce-scatter.6.cloned.1.call-update
  95.1 0.0 reduce-scatter.12.cloned.1.call-start
  95.1 1.4 convolution_convert_fusion.1
  96.5 0.0 reduce-scatter.12.cloned.1.call-update
  96.5 0.0 reduce-scatter.14.cloned.1.call-start
  96.6 0.0 copy-start.5
  96.6 2.6 %fusion.22 = bf16[1,192,2048]{2,1,0:T(8,128)(2,1)} fusion(bf16[1,1,192,2048]{3,2,1,0:T(8,128)(2,1)S(1)} %copy-done.1, f32[192,2048]{1,0:T(8,128)S(1)} %get-tuple-element.13, f32[192]{0:T(256)S(1)} %broadcast_multiply_fusion, f32[192]{0:T(256)S(1)} %get-tuple-element.8, f32[192]{0:T(256)S(1)} %get-tuple-element.9, bf16[1,1,192,2048]{3,2,1,0:T(8,128)(2,1)} %param.9, ...), kind=kLoop, calls=%fused_computation.31 | loop fusion | flops 3538944 | bytes 3934656 | tf_op jit(solution)/shard_map/stack | solution.py:109
  99.2 0.0 copy-start.3
  99.2 0.0 copy-start.6
  99.2 1.4 collective-permute-start.1
  100.6 7.4 %all_gather.11 = bf16[192,192]{0,1:T(8,128)(2,1)S(1)} all-gather(bf16[192,48]{0,1:T(8,128)(2,1)S(1)} %get-tuple-element.6), channel_id=1, replica_groups=mesh['section'=4,'tensor'=4,'dp'=2] {'tensor'}, dimensions={1}, use_global_device_ids=true | all-gather | bytes 92160 | tf_op jit(solution)/shard_map/all_gather | solution.py:89
  108.0 0.0 copy-done.5
  108.0 1.3 convolution_convert_fusion
  109.4 0.0 reduce-scatter.14.cloned.1.call-update
  109.4 9.1 %reduce-scatter.6.cloned.1.call-done = bf16[192,48]{0,1:T(8,128)(2,1)} async-done(((bf16[192,192]{0,1:T(8,128)(2,1)}), bf16[192,48]{0,1:T(8,128)(2,1)}) %reduce-scatter.6.cloned.1.call-update) | async-done | bytes 18448 | tf_op jit(solution)/shard_map/reduce_scatter | solution.py:75
  118.5 0.8 fusion.45
  119.2 8.4 %all_gather.9 = bf16[192,192]{0,1:T(8,128)(2,1)S(1)} all-gather(bf16[192,48]{0,1:T(8,128)(2,1)S(1)} %fusion.45), channel_id=1, replica_groups=mesh['section'=4,'tensor'=4,'dp'=2] {'tensor'}, dimensions={1}, use_global_device_ids=true | all-gather | bytes 92160 | tf_op jit(solution)/shard_map/all_gather | solution.py:86
  127.6 0.0 copy-done.3
  127.6 0.0 copy-done.6
  127.6 0.4 fusion.1
  128.0 3.5 %collective-permute-start = (bf16[1,192,2048]{2,1,0:T(8,128)(2,1)S(1)}, bf16[1,192,2048]{2,1,0:T(8,128)(2,1)S(1)}, u32[]{:S(2)}, u32[]{:S(2)}) collective-permute-start(bf16[1,192,2048]{2,1,0:T(8,128)(2,1)S(1)} %fusion.1), channel_id=1, source_target_pairs={{0,8},{8,16},{16,24},{1,9},{9,17},{17,25},{2,10},{10,18},{18,26},{... | collective-permute-start | bytes 2359304 | tf_op jit(solution)/shard_map/ppermute | solution.py:17
  131.5 0.0 collective-permute-done.1
  131.5 14.1 %collective-permute-done = bf16[1,192,2048]{2,1,0:T(8,128)(2,1)S(1)} collective-permute-done((bf16[1,192,2048]{2,1,0:T(8,128)(2,1)S(1)}, bf16[1,192,2048]{2,1,0:T(8,128)(2,1)S(1)}, u32[]{:S(2)}, u32[]{:S(2)}) %collective-permute-start) | collective-permute-done | bytes 786464 | tf_op jit(solution)/shard_map/ppermute | solution.py:17
  145.7 0.0 reduce-scatter.12.cloned.1.call-done
  145.7 1.8 %fusion.39 = bf16[1,96,2048]{2,1,0:T(8,128)(2,1)} fusion(bf16[96,2048]{1,0:T(8,128)(2,1)} %reduce-scatter.12.cloned.1.call-done), kind=kLoop, calls=%fused_computation.50 | loop fusion | flops 589824 | bytes 786432 | tf_op jit(solution)/shard_map/broadcast_in_dim | solution.py:124
  147.5 0.0 reduce-scatter.14.cloned.1.call-done
  147.5 1.8 %fusion.40 = bf16[1,96,2048]{2,1,0:T(8,128)(2,1)} fusion(bf16[96,2048]{1,0:T(8,128)(2,1)} %reduce-scatter.14.cloned.1.call-done), kind=kLoop, calls=%fused_computation.51 | loop fusion | flops 589824 | bytes 786432 | tf_op jit(solution)/shard_map/broadcast_in_dim | solution.py:124
  149.3 0.9 copy.13
  150.2 0.9 copy.14
  (3 shorter events, 0.0 us)
Async XLA Ops:
  7.2 13.7 %copy-start = (bf16[1,192,2048]{2,1,0:T(8,128)(2,1)S(1)}, bf16[1,192,2048]{2,1,0:T(8,128)(2,1)}, u32[]{:S(2)}) copy-start(bf16[1,192,2048]{2,1,0:T(8,128)(2,1)} %param.12) | copy-start | bytes 2359300
  7.2 39.6 %reduce-scatter.10.cloned.1.call-start = ((), (), s32[]{:S(2)}) async-start(), calls=%async_computation.7 | async-start | bytes 122880 | tf_op jit(solution)/shard_map/reduce_scatter | solution.py:78
  8.0 15.2 %copy-start.7 = (s32[1,1,2]{2,1,0:T(1,128)S(1)}, s32[1,1,2]{2,1,0:T(1,128)}, u32[]{:S(2)}) copy-start(s32[1,1,2]{2,1,0:T(1,128)} %param.10) | copy-start | bytes 28
  8.0 17.1 %copy-start.4 = (bf16[1,1,192,2048]{3,2,1,0:T(8,128)(2,1)S(1)}, bf16[1,1,192,2048]{3,2,1,0:T(8,128)(2,1)}, u32[]{:S(2)}) copy-start(bf16[1,1,192,2048]{3,2,1,0:T(8,128)(2,1)} %param.9) | copy-start | bytes 2359300
  23.1 4.4 %copy-start.2 = (bf16[1,1,192,2048]{3,2,1,0:T(8,128)(2,1)S(1)}, bf16[1,1,192,2048]{3,2,1,0:T(8,128)(2,1)}, u32[]{:S(2)}) copy-start(bf16[1,1,192,2048]{3,2,1,0:T(8,128)(2,1)} %param.7) | copy-start | bytes 2359300
  23.1 51.1 %reduce-scatter.8.cloned.1.call-start = ((), (), s32[]{:S(2)}) async-start(), calls=%async_computation.6 | async-start | bytes 122880 | tf_op jit(solution)/shard_map/reduce_scatter | solution.py:81
  25.1 58.3 %copy-start.1 = (bf16[1,1,192,2048]{3,2,1,0:T(8,128)(2,1)S(1)}, bf16[1,1,192,2048]{3,2,1,0:T(8,128)(2,1)}, u32[]{:S(2)}) copy-start(bf16[1,1,192,2048]{3,2,1,0:T(8,128)(2,1)} %param.8) | copy-start | bytes 2359300
  27.5 91.0 %reduce-scatter.6.cloned.1.call-start = ((), (), s32[]{:S(2)}) async-start(), calls=%async_computation.5 | async-start | bytes 122880 | tf_op jit(solution)/shard_map/reduce_scatter | solution.py:75
  95.1 50.6 %reduce-scatter.12.cloned.1.call-start = ((), (), s32[]{:S(2)}) async-start(), calls=%async_computation.8 | async-start | bytes 1179648 | tf_op jit(solution)/shard_map/reduce_scatter | solution.py:114
  96.5 51.0 %reduce-scatter.14.cloned.1.call-start = ((), (), s32[]{:S(2)}) async-start(), calls=%async_computation.9 | async-start | bytes 1179648 | tf_op jit(solution)/shard_map/reduce_scatter | solution.py:117
  96.6 11.5 %copy-start.5 = (bf16[1,1,192,2048]{3,2,1,0:T(8,128)(2,1)S(1)}, bf16[1,1,192,2048]{3,2,1,0:T(8,128)(2,1)}, u32[]{:S(2)}) copy-start(bf16[1,1,192,2048]{3,2,1,0:T(8,128)(2,1)} %param.9) | copy-start | bytes 2359300
  99.2 28.4 %copy-start.3 = (bf16[1,1,192,2048]{3,2,1,0:T(8,128)(2,1)S(1)}, bf16[1,1,192,2048]{3,2,1,0:T(8,128)(2,1)}, u32[]{:S(2)}) copy-start(bf16[1,1,192,2048]{3,2,1,0:T(8,128)(2,1)} %param.7) | copy-start | bytes 2359300
  99.2 28.4 %copy-start.6 = (bf16[1,192,2048]{2,1,0:T(8,128)(2,1)S(1)}, bf16[1,192,2048]{2,1,0:T(8,128)(2,1)}, u32[]{:S(2)}) copy-start(bf16[1,192,2048]{2,1,0:T(8,128)(2,1)} %param.13) | copy-start | bytes 2359300
  99.2 32.3 %collective-permute-start.1 = (bf16[1,192,2048]{2,1,0:T(8,128)(2,1)}, bf16[1,192,2048]{2,1,0:T(8,128)(2,1)S(1)}, u32[]{:S(2)}, u32[]{:S(2)}) collective-permute-start(bf16[1,192,2048]{2,1,0:T(8,128)(2,1)} %fusion.22), channel_id=1, source_target_pairs={{8,0},{16,8},{24,16},{9,1},{17,9},{25,17},{10,2},{18,10},{26,18},{... | collective-permute-start | bytes 2359304 | tf_op jit(solution)/shard_map/ppermute | solution.py:19
  128.0 17.7 %collective-permute-start = (bf16[1,192,2048]{2,1,0:T(8,128)(2,1)S(1)}, bf16[1,192,2048]{2,1,0:T(8,128)(2,1)S(1)}, u32[]{:S(2)}, u32[]{:S(2)}) collective-permute-start(bf16[1,192,2048]{2,1,0:T(8,128)(2,1)S(1)} %fusion.1), channel_id=1, source_target_pairs={{0,8},{8,16},{16,24},{1,9},{9,17},{17,25},{2,10},{10,18},{18,26},{... | collective-permute-start | bytes 2359304 | tf_op jit(solution)/shard_map/ppermute | solution.py:17
Sparse Core Ops, SparseCore 0:
  23.3 23.4 reduce-scatter.9
  50.1 24.1 reduce-scatter.7
  95.2 23.2 reduce-scatter.5
  121.1 8.1 reduce-scatter.11
  131.4 9.2 reduce-scatter.13
where the time goes:
time: 158 us
  waiting for transfers between devices  69.8 us (44%)
  blocking collectives  44.4 us (28%)
  between operations  13.9 us (9%)
  other arithmetic  11.6 us (7%)
  matrix products  10.4 us (7%)
  starting transfers between devices  5.13 us (3%)
  local copies, waits for them, and re-layouts  2.39 us (2%)
    reduce_scatter x1, waiting for transfers between devices, shards(): lax.psum_scatter(slope_part.astype(jnp.bfloat16), 'tensor', scatter_dimen...  27.5 us
    psum x2, blocking collectives, shards(): lax.psum((jnp.sum(forward_values * forward_values, axis=1), jnp.sum(saved...  20.3 us
    reduce_scatter x1, waiting for transfers between devices, shards(): lax.psum_scatter(saved_part.astype(jnp.bfloat16), 'tensor', scatter_dimen...  19 us
    ppermute x1, waiting for transfers between devices, padded_2(): lax.ppermute(tail, axis, [(i, (i + 1) % count) for i in range(ends)])  14.1 us
    reduce_scatter x1, waiting for transfers between devices, shards(): lax.psum_scatter(forward_part.astype(jnp.bfloat16), 'tensor', scatter_dim...  9.06 us
    all_gather x1, blocking collectives, shards(): lax.all_gather(jax.nn.silu(forward_share).astype(jnp.bfloat16), 'tensor',...  8.36 us
    all_gather x1, blocking collectives, shards(): lax.all_gather((slope_share * silu_slope(saved_share)).astype(jnp.bfloat1...  8.3 us
    all_gather x1, blocking collectives, shards(): lax.all_gather(jax.nn.silu(saved_share).astype(jnp.bfloat16), 'tensor', a...  7.44 us
  transfers between devices with their start and end apart: 7, of which 4 were waited for; matrix products, arithmetic and copies ran while one was open for 8% of the time, Pallas kernels for 0%

commit v1 on v0

v1 whole, which is shorter than its diff:
```python
import functools

import jax
import jax.numpy as jnp
from jax import lax
from jax.experimental import pallas as pl
from jax.experimental.pallas import tpu as pltpu
from jax.sharding import PartitionSpec as P

EPSILON = 1e-05
LANES = 128
F32 = jnp.float32
BF16 = jnp.bfloat16


def round_up(value, unit):
    return -(-value // unit) * unit


def partner(index, step, count):
    if count & (count - 1) == 0:
        return index ^ step
    return (index + step) % count


def source(index, step, count):
    if count & (count - 1) == 0:
        return index ^ step
    return (index - step + count) % count


def send_step(cells, axis, step):
    count = lax.axis_size(axis)
    return lax.ppermute(cells, axis, [(i, partner(i, step, count)) for i in range(count)])


def contract_last(left_side, right_side):
    return lax.dot_general(left_side, right_side, (((1,), (1,)), ((), ())), preferred_element_type=F32)


def contract_rows(left_side, right_side):
    return lax.dot_general(left_side, right_side, (((0,), (0,)), ((), ())), preferred_element_type=F32)


def split_pair(values):
    high = values.astype(BF16).astype(F32)
    return high, values - high


def place_pair(slot, unit_count, pair):
    lane = lax.broadcasted_iota(jnp.int32, slot.shape, 1)
    high, low = pair
    rest = jnp.where(lane == unit_count, high, jnp.where(lane == unit_count + 1, low, 0.0))
    return jnp.where(lane < unit_count, slot, rest)


def take_pair(slot, unit_count):
    return slot[:, unit_count : unit_count + 1] + slot[:, unit_count + 1 : unit_count + 2]


def keep_mask(first_row, shape, seq_rows, lengths_ref):
    row = first_row + lax.broadcasted_iota(jnp.int32, shape, 0)
    limit = jnp.where(row < seq_rows, lengths_ref[0], lengths_ref[1] + seq_rows)
    return row < limit


def partials_body(unit_count, slot, share_count, place_ref, fwd_ref, saved_ref, grad_ref, gain_ref, down_ref, up_ref, *refs):
    outs = refs[:share_count]
    acc_ref, squares_ref = refs[share_count:]
    step = pl.program_id(0)

    @pl.when(step == 0)
    def _():
        acc_ref[...] = jnp.zeros_like(acc_ref)
        squares_ref[...] = jnp.zeros_like(squares_ref)

    gain = gain_ref[...].astype(F32)
    down = down_ref[...]
    for which, rows_ref in enumerate((fwd_ref, saved_ref)):
        values = rows_ref[...].astype(F32)
        lo = which * slot
        acc_ref[:, lo : lo + unit_count] += contract_last((values * gain).astype(BF16), down)
        total = squares_ref[which]
        for c in range(0, values.shape[1], LANES):
            part = values[:, c : c + LANES]
            total += part * part
        squares_ref[which] = total
    acc_ref[:, 2 * slot : 2 * slot + unit_count] += contract_last(grad_ref[...], up_ref[...])

    @pl.when(step == pl.num_programs(0) - 1)
    def _():
        for which in range(2):
            total = jnp.sum(squares_ref[which], axis=1, keepdims=True)
            lo = which * slot
            acc_ref[:, lo : lo + slot] = place_pair(acc_ref[:, lo : lo + slot], unit_count, split_pair(total))
        share_rows = outs[0].shape[0]
        for k, out in enumerate(outs):
            first = pl.multiple_of(partner(place_ref[0], k, share_count) * share_rows, share_rows)
            out[...] = acc_ref[pl.ds(first, share_rows), :].astype(BF16)


def middle_body(unit_count, slot, full_width, seq_rows, place_ref, lengths_ref, *refs):
    parts, out = refs[:-1], refs[-1]
    total = parts[0][...].astype(F32)
    for part in parts[1:]:
        total += part[...].astype(F32)
    share_rows = total.shape[0]
    keep = keep_mask(place_ref[0] * share_rows, (share_rows, slot), seq_rows, lengths_ref)
    fwd, saved, slope = (total[:, i * slot : (i + 1) * slot] for i in range(3))
    fwd_scale = lax.rsqrt(take_pair(fwd, unit_count) / full_width + EPSILON)
    saved_scale = lax.rsqrt(take_pair(saved, unit_count) / full_width + EPSILON)
    lane = lax.broadcasted_iota(jnp.int32, fwd.shape, 1)
    unit = lane < unit_count
    fwd_rank = fwd * fwd_scale
    saved_rank = saved * saved_scale
    gate = jax.nn.sigmoid(saved_rank)
    back = jnp.where(unit & keep, slope * (gate * (1.0 + saved_rank * (1.0 - gate))), 0.0)
    bend = saved_scale * saved_scale * (jnp.sum(back * saved_rank, axis=1, keepdims=True) / full_width)
    out[:, 0:slot] = jnp.where(unit, fwd_rank * jax.nn.sigmoid(fwd_rank), 0.0).astype(BF16)
    out[:, slot : 2 * slot] = jnp.where(unit & keep, saved_rank * gate, 0.0).astype(BF16)
    out[:, 2 * slot :] = place_pair(back * saved_scale, unit_count, split_pair(bend)).astype(BF16)


def join_shares(place_ref, shares, whole_ref):
    share_rows = shares[0].shape[0]
    for k, share in enumerate(shares):
        first = source(place_ref[0], k, len(shares)) * share_rows
        whole_ref[pl.ds(pl.multiple_of(first, share_rows), share_rows), :] = share[...]


def edges_body(unit_count, slot, share_count, seq_rows, place_ref, lengths_ref, *refs):
    shares = refs[:share_count]
    fwd_ref, saved_ref, grad_ref, gain_ref, down_ref, up_ref, out_fwd, out_grad, whole_ref = refs[share_count:]

    @pl.when(pl.program_id(0) == 0)
    def _():
        join_shares(place_ref, shares, whole_ref)

    keep = keep_mask(0, grad_ref.shape, seq_rows, lengths_ref)
    back = whole_ref[:, 2 * slot : 2 * slot + unit_count]
    bend = take_pair(whole_ref[:, 2 * slot :].astype(F32), unit_count)
    weighted = jnp.dot(back, down_ref[...], preferred_element_type=F32) * gain_ref[...].astype(F32)
    kept = jnp.where(keep, grad_ref[...].astype(F32), 0.0)
    out_grad[...] = (kept + weighted - saved_ref[...].astype(F32) * bend).astype(BF16)
    act = whole_ref[:, 0:unit_count]
    lifted = jnp.dot(act, up_ref[...], preferred_element_type=F32)
    out_fwd[...] = (fwd_ref[...].astype(F32) + lifted).astype(BF16)


def grads_body(unit_count, slot, share_count, place_ref, *refs):
    shares = refs[:share_count]
    saved_ref, grad_ref, gain_ref = refs[share_count : share_count + 3]
    outs = refs[share_count + 3 : -2]
    whole_ref, hold_ref = refs[-2:]

    @pl.when(pl.program_id(0) == 0)
    def _():
        join_shares(place_ref, shares, whole_ref)

    back = whole_ref[:, 2 * slot : 2 * slot + unit_count]
    act = whole_ref[:, slot : slot + unit_count]
    hold_ref[0] = contract_rows(back, saved_ref[...]) * gain_ref[...].astype(F32)
    hold_ref[1] = contract_rows(act, grad_ref[...])
    group_count = len(outs)
    group_rows = unit_count // group_count
    for k, out in enumerate(outs):
        first = partner(place_ref[1], k, group_count) * group_rows
        for which in range(2):
            out[which] = hold_ref[which, pl.ds(pl.multiple_of(first, group_rows), group_rows), :].astype(BF16)


def shards(forward_rows, saved_rows, output_grad, lengths, norm_gain, down_map, up_map):
    fwd, saved, grad = forward_rows[0, 0], saved_rows[0, 0], output_grad[0, 0]
    seq_lengths = lengths[0, 0]
    down, up = down_map[0], up_map[0]
    row_count, width = fwd.shape
    unit_count = down.shape[0]
    share_count = lax.axis_size("tensor")
    group_count = lax.axis_size("dp")
    section_count = lax.axis_size("section")
    share_rows = row_count // share_count
    seq_rows = row_count // 2
    full_width = width * share_count
    slot = round_up(unit_count + 2, LANES)
    packed = 3 * slot
    place = jnp.stack([lax.axis_index("tensor"), lax.axis_index("dp")]).astype(jnp.int32)
    block = min(width, 512)
    steps = width // block
    smem = pl.BlockSpec(memory_space=pltpu.SMEM)
    cols = lambda n: pl.BlockSpec((n, block), lambda j: (0, j))
    whole = pl.BlockSpec((share_rows, packed), lambda j: (0, 0))
    share_type = jax.ShapeDtypeStruct((share_rows, packed), BF16)

    parts = pl.pallas_call(
        functools.partial(partials_body, unit_count, slot, share_count),
        grid=(steps,),
        in_specs=[smem, cols(row_count), cols(row_count), cols(row_count), cols(1), cols(unit_count), cols(unit_count)],
        out_specs=[whole] * share_count,
        out_shape=[share_type] * share_count,
        scratch_shapes=[pltpu.VMEM((row_count, packed), F32), pltpu.VMEM((2, row_count, LANES), F32)],
        name="partials",
    )(place, fwd, saved, grad, norm_gain, down, up)
    got = [parts[0]] + [send_step(parts[k], "tensor", k) for k in range(1, share_count)]
    mine = pl.pallas_call(
        functools.partial(middle_body, unit_count, slot, full_width, seq_rows),
        in_specs=[smem, smem] + [pl.BlockSpec(memory_space=pltpu.VMEM)] * share_count,
        out_specs=pl.BlockSpec(memory_space=pltpu.VMEM),
        out_shape=share_type,
        name="middle",
    )(place, seq_lengths, *got)
    shares = [mine] + [send_step(mine, "tensor", k) for k in range(1, share_count)]
    out_fwd, out_grad = pl.pallas_call(
        functools.partial(edges_body, unit_count, slot, share_count, seq_rows),
        grid=(steps,),
        in_specs=[smem, smem] + [whole] * share_count
        + [cols(row_count), cols(row_count), cols(row_count), cols(1), cols(unit_count), cols(unit_count)],
        out_specs=[cols(row_count)] * 2,
        out_shape=[jax.ShapeDtypeStruct((row_count, width), BF16)] * 2,
        scratch_shapes=[pltpu.VMEM((row_count, packed), BF16)],
        name="edges",
    )(place, seq_lengths, *shares, fwd, saved, grad, norm_gain, down, up)
    next_grads = lax.ppermute(out_grad, "section", [(i + 1, i) for i in range(section_count - 1)])
    next_inputs = lax.ppermute(out_fwd, "section", [(i, i + 1) for i in range(section_count - 1)])
    group_rows = unit_count // group_count
    halves = pl.pallas_call(
        functools.partial(grads_body, unit_count, slot, share_count),
        grid=(steps,),
        in_specs=[smem] + [whole] * share_count + [cols(row_count), cols(row_count), cols(1)],
        out_specs=[pl.BlockSpec((2, group_rows, block), lambda j: (0, 0, j))] * group_count,
        out_shape=[jax.ShapeDtypeStruct((2, group_rows, width), BF16)] * group_count,
        scratch_shapes=[pltpu.VMEM((row_count, packed), BF16), pltpu.VMEM((2, unit_count, block), F32)],
        name="grads",
    )(place, *shares, saved, grad, norm_gain)
    total = halves[0].astype(F32)
    for k in range(1, group_count):
        total += send_step(halves[k], "dp", k).astype(F32)
    mean = (total * (1.0 / group_count)).astype(BF16)
    return (next_inputs[None, None], next_grads[None, None], mean[0:1], mean[1:2])


def solution(mesh):
    rows = P("section", "dp", None, "tensor")
    maps = P("section", None, "tensor")
    return jax.shard_map(
        shards,
        mesh=mesh,
        in_specs=(rows, rows, rows, P("section", "dp", None), P("section", "tensor"), maps, maps),
        out_specs=(rows, rows, P("section", "dp", "tensor"), P("section", "dp", "tensor")),
        check_vma=False,
    )
```

time: 158 us -> 62.9 us (0.40)
  blocking collectives: 44.4 us -> 0 us
  waiting for transfers between devices: 69.8 us -> 26.7 us
  Pallas kernels: 0 us -> 16.1 us
  between operations: 13.9 us -> 0.7 us
  matrix products: 10.4 us -> 0 us
  other arithmetic: 11.6 us -> 2.08 us
  starting transfers between devices: 5.13 us -> 13 us
  local copies, waits for them, and re-layouts: 2.39 us -> 3.97 us
    reduce_scatter x5 -> x0, waiting for transfers between devices: 55.6 us -> none  [the longest x1 27.5 us: shards(): lax.psum_scatter(slope_part.astype(jnp.bfloat16), 'tensor', scatter_dimen...]
    all_gather x3 -> x0, blocking collectives: 24.1 us -> none  [the longest x1 8.36 us: shards(): lax.all_gather(jax.nn.silu(forward_share).astype(jnp.bfloat16), 'tensor',...]
    psum x2 -> x0, blocking collectives: 20.3 us -> none  [shards(): lax.psum((jnp.sum(forward_values * forward_values, axis=1), jnp.sum(saved...]
    pallas_call x0 -> x4, Pallas kernels: none -> 16.1 us  [the longest x1 4.76 us: shards(): pl.pallas_call(functools.partial(edges_body, unit_count, slot, share_coun...]
    ppermute x2 -> x9, waiting for transfers between devices: 14.1 us -> 26.7 us  [the longest x1 9.79 us: shards(): lax.ppermute(out_grad, 'section', [(i + 1, i) for i in range(section_coun...]
    dot_general x7 -> x0, matrix products: 10.4 us -> none  [the longest x3 6.81 us: contract_last(): lax.dot_general(left_side, right_side, (((1,), (1,)), ((), ())), preferre...]
    ppermute x2 -> x9, starting transfers between devices: 4.92 us -> 13 us  [the longest x7 8.03 us: send_step(): lax.ppermute(cells, axis, [(i, partner(i, step, count)) for i in range(co...]
    broadcast_in_dim x2 -> x0, other arithmetic: 3.62 us -> none  [the longest x1 1.81 us: shards(): grad_down[None]]
  transfers between devices with their start and end apart: 7 -> 9, of which waited for: 4 -> 8; matrix products, arithmetic and copies ran while one was open for 8% -> 4% of each run, Pallas kernels for 0% -> 7%
where the time goes in v1:
time: 62.9 us; the launch traced here: 62.5 us
  waiting for transfers between devices  26.7 us (42%)
  Pallas kernels  16.1 us (26%)
  starting transfers between devices  13 us (21%)
  local copies, waits for them, and re-layouts  3.97 us (6%)
  other arithmetic  2.08 us (3%)
  between operations  0.7 us (1%)
    ppermute x1, waiting for transfers between devices, shards(): lax.ppermute(out_grad, 'section', [(i + 1, i) for i in range(section_coun...  9.79 us
    ppermute x7, waiting for transfers between devices, send_step(): lax.ppermute(cells, axis, [(i, partner(i, step, count)) for i in range(co...  8.51 us
    ppermute x1, waiting for transfers between devices, shards(): lax.ppermute(out_fwd, 'section', [(i, i + 1) for i in range(section_count...  8.39 us
    ppermute x7, starting transfers between devices, send_step(): lax.ppermute(cells, axis, [(i, partner(i, step, count)) for i in range(co...  8.03 us
    pallas_call x1, Pallas kernels, shards(): pl.pallas_call(functools.partial(edges_body, unit_count, slot, share_coun...  4.76 us
    pallas_call x1, Pallas kernels, shards(): pl.pallas_call(functools.partial(grads_body, unit_count, slot, share_coun...  4.68 us
    pallas_call x1, Pallas kernels, shards(): pl.pallas_call(functools.partial(partials_body, unit_count, slot, share_c...  4.65 us
    ppermute x1, starting transfers between devices, shards(): lax.ppermute(out_fwd, 'section', [(i, i + 1) for i in range(section_count...  3.66 us
  transfers between devices with their start and end apart: 9, of which 8 were waited for; matrix products, arithmetic and copies ran while one was open for 4% of the time, Pallas kernels for 7%

profile of v1, /device:TPU:0, one launch (start us, length us, event | category | flops | bytes accessed | tf_op | source)
XLA Modules:
  0.0 62.5 jit_solution(9874670752991903785)
XLA Ops:
  0.6 0.7 %pad_add_fusion.place_ref = s32[2]{0:T(128)} fusion(s32[1]{0:T(128)} %bitcast.1, s32[1]{0:T(128)} %bitcast), kind=kLoop, calls=%fused_computation.1 | loop fusion | flops 2 | bytes 16 | tf_op jit(solution)/shard_map/stack | solution.py:186
  1.3 4.7 %partials.1 = (bf16[48,768]{1,0:T(8,128)(2,1)}, bf16[48,768]{1,0:T(8,128)(2,1)}, bf16[48,768]{1,0:T(8,128)(2,1)}, bf16[48,768]{1,0:T(8,128)(2,1)}) custom-call(s32[2]{0:T(128)} %pad_add_fusion.place_ref, bf16[192,2048]{1,0:T(8,128)(2,1)} %bitcast.16, bf16[192,2048]{1,0:T(8,128)(2,1)} %bitcast.10, bf16[192,2048]{1,0:T(8,128)(2,1)} %bitcast.13, ...), custom_call_target="tpu_custom_call" | custom-call | tf_op jit(solution)/shard_map/partials/pallas_call | solution.py:194
  5.9 3.0 %collective-permute-start = (bf16[48,768]{1,0:T(8,128)(2,1)}, bf16[48,768]{1,0:T(8,128)(2,1)S(1)}, u32[]{:S(2)}, u32[]{:S(2)}) collective-permute-start(bf16[48,768]{1,0:T(8,128)(2,1)} %get-tuple-element.13), channel_id=1, source_target_pairs={{0,2},{2,0},{4,6},{6,4},{1,3},{3,1},{5,7},{7,5},{8,10},{10,8},{12,... | collective-permute-start | bytes 221192 | tf_op jit(solution)/shard_map/ppermute | solution.py:34
  8.9 1.5 %collective-permute-start.1 = (bf16[48,768]{1,0:T(8,128)(2,1)}, bf16[48,768]{1,0:T(8,128)(2,1)S(1)}, u32[]{:S(2)}, u32[]{:S(2)}) collective-permute-start(bf16[48,768]{1,0:T(8,128)(2,1)} %get-tuple-element.14), channel_id=1, source_target_pairs={{0,4},{2,6},{4,0},{6,2},{1,5},{3,7},{5,1},{7,3},{8,12},{10,14},{12... | collective-permute-start | bytes 221192 | tf_op jit(solution)/shard_map/ppermute | solution.py:34
  10.5 0.0 collective-permute-start.2
  10.5 1.3 %collective-permute-done.refs_1_ = bf16[48,768]{1,0:T(8,128)(2,1)S(1)} collective-permute-done((bf16[48,768]{1,0:T(8,128)(2,1)}, bf16[48,768]{1,0:T(8,128)(2,1)S(1)}, u32[]{:S(2)}, u32[]{:S(2)}) %collective-permute-start) | collective-permute-done | bytes 73760 | tf_op jit(solution)/shard_map/ppermute | solution.py:34
  11.8 0.0 copy-start.3
  11.8 1.7 %collective-permute-done.1.refs_2_ = bf16[48,768]{1,0:T(8,128)(2,1)S(1)} collective-permute-done((bf16[48,768]{1,0:T(8,128)(2,1)}, bf16[48,768]{1,0:T(8,128)(2,1)S(1)}, u32[]{:S(2)}, u32[]{:S(2)}) %collective-permute-start.1) | collective-permute-done | bytes 73760 | tf_op jit(solution)/shard_map/ppermute | solution.py:34
  13.5 0.0 copy-start.4
  13.5 2.4 %collective-permute-done.2.refs_3_ = bf16[48,768]{1,0:T(8,128)(2,1)S(1)} collective-permute-done((bf16[48,768]{1,0:T(8,128)(2,1)}, bf16[48,768]{1,0:T(8,128)(2,1)S(1)}, u32[]{:S(2)}, u32[]{:S(2)}) %collective-permute-start.2) | collective-permute-done | bytes 73760 | tf_op jit(solution)/shard_map/ppermute | solution.py:34
  15.9 0.0 copy-start.5
  15.9 0.0 copy-done.3
  15.9 0.0 copy-done.4
  15.9 0.6 %copy-done.5 = bf16[48,768]{1,0:T(8,128)(2,1)} copy-done((bf16[48,768]{1,0:T(8,128)(2,1)}, bf16[48,768]{1,0:T(8,128)(2,1)S(1)}, u32[]{:S(2)}) %copy-start.5) | copy-done | bytes 73752
  16.6 2.0 %middle.1.refs_0_ = bf16[48,768]{1,0:T(8,128)(2,1)} custom-call(s32[2]{0:T(128)} %pad_add_fusion.place_ref, s32[2]{0:T(128)} %bitcast.24, bf16[48,768]{1,0:T(8,128)(2,1)} %get-tuple-element.12.refs_0_, bf16[48,768]{1,0:T(8,128)(2,1)} %copy-done.3, bf16[48,768]{1,0:T(8,128)(2,1)} %copy-done.4, bf16[48,768]{1,0:T(8,128)(2,1)} %copy-done.5), custom_call_target="tpu_custom_call" | custom-call | tf_op jit(solution)/shard_map/middle/pallas_call | solution.py:204
  18.5 0.4 collective-permute-start.5
  19.0 1.6 %collective-permute-start.4 = (bf16[48,768]{1,0:T(8,128)(2,1)}, bf16[48,768]{1,0:T(8,128)(2,1)S(1)}, u32[]{:S(2)}, u32[]{:S(2)}) collective-permute-start(bf16[48,768]{1,0:T(8,128)(2,1)} %middle.1.refs_0_), channel_id=1, source_target_pairs={{0,4},{2,6},{4,0},{6,2},{1,5},{3,7},{5,1},{7,3},{8,12},{10,14},{12... | collective-permute-start | bytes 221192 | tf_op jit(solution)/shard_map/ppermute | solution.py:34
  20.5 1.5 %collective-permute-start.3 = (bf16[48,768]{1,0:T(8,128)(2,1)}, bf16[48,768]{1,0:T(8,128)(2,1)S(1)}, u32[]{:S(2)}, u32[]{:S(2)}) collective-permute-start(bf16[48,768]{1,0:T(8,128)(2,1)} %middle.1.refs_0_), channel_id=1, source_target_pairs={{0,2},{2,0},{4,6},{6,4},{1,3},{3,1},{5,7},{7,5},{8,10},{10,8},{12,... | collective-permute-start | bytes 221192 | tf_op jit(solution)/shard_map/ppermute | solution.py:34
  22.0 2.1 %collective-permute-done.5.refs_3_ = bf16[48,768]{1,0:T(8,128)(2,1)S(1)} collective-permute-done((bf16[48,768]{1,0:T(8,128)(2,1)}, bf16[48,768]{1,0:T(8,128)(2,1)S(1)}, u32[]{:S(2)}, u32[]{:S(2)}) %collective-permute-start.5) | collective-permute-done | bytes 73760 | tf_op jit(solution)/shard_map/ppermute | solution.py:34
  24.1 0.0 copy-start
  24.1 0.2 collective-permute-done.4.refs_2_
  24.3 0.0 copy-start.1
  24.3 0.8 %collective-permute-done.3.refs_1_ = bf16[48,768]{1,0:T(8,128)(2,1)S(1)} collective-permute-done((bf16[48,768]{1,0:T(8,128)(2,1)}, bf16[48,768]{1,0:T(8,128)(2,1)S(1)}, u32[]{:S(2)}, u32[]{:S(2)}) %collective-permute-start.3) | collective-permute-done | bytes 73760 | tf_op jit(solution)/shard_map/ppermute | solution.py:34
  25.1 0.0 copy-done
  25.1 0.0 copy-done.1
  25.1 0.0 copy-start.2
  25.1 0.6 %copy-done.2 = bf16[48,768]{1,0:T(8,128)(2,1)} copy-done((bf16[48,768]{1,0:T(8,128)(2,1)}, bf16[48,768]{1,0:T(8,128)(2,1)S(1)}, u32[]{:S(2)}) %copy-start.2) | copy-done | bytes 73752
  25.7 4.8 %edges.1 = (bf16[192,2048]{1,0:T(8,128)(2,1)}, bf16[192,2048]{1,0:T(8,128)(2,1)}) custom-call(s32[2]{0:T(128)} %pad_add_fusion.place_ref, s32[2]{0:T(128)} %bitcast.25, bf16[48,768]{1,0:T(8,128)(2,1)} %middle.1.refs_0_, bf16[48,768]{1,0:T(8,128)(2,1)} %copy-done.2, bf16[48,768]{1,0:T(8,128)(2,1)} %copy-done.1, bf16[48,768]{1,0:T(8,128)(2,1)} %copy-done, ...), custom_call_target="tpu_custom_call" | custom-call | tf_op jit(solution)/shard_map/edges/pallas_call | solution.py:212
  30.5 0.0 copy-start.6
  30.5 3.7 %collective-permute-start.6 = (bf16[192,2048]{1,0:T(8,128)(2,1)}, bf16[192,2048]{1,0:T(8,128)(2,1)S(1)}, u32[]{:S(2)}, u32[]{:S(2)}) collective-permute-start(bf16[192,2048]{1,0:T(8,128)(2,1)} %get-tuple-element.16), channel_id=1, source_target_pairs={{0,8},{8,16},{16,24},{1,9},{9,17},{17,25},{2,10},{10,18},{18,26},{... | collective-permute-start | bytes 2359304 | tf_op jit(solution)/shard_map/ppermute | solution.py:223
  34.2 4.7 %grads.1 = (bf16[2,96,2048]{2,1,0:T(8,128)(2,1)}, bf16[2,96,2048]{2,1,0:T(8,128)(2,1)}) custom-call(s32[2]{0:T(128)} %pad_add_fusion.place_ref, bf16[48,768]{1,0:T(8,128)(2,1)} %middle.1.refs_0_, bf16[48,768]{1,0:T(8,128)(2,1)} %copy-done.2, bf16[48,768]{1,0:T(8,128)(2,1)} %copy-done.1, bf16[48,768]{1,0:T(8,128)(2,1)} %copy-done, ...), custom_call_target="tpu_custom_call" | custom-call | tf_op jit(solution)/shard_map/grads/pallas_call | solution.py:225
  38.9 0.0 collective-permute-start.8
  38.9 0.0 copy-done.6
  38.9 1.3 %collective-permute-start.7 = (bf16[192,2048]{1,0:T(8,128)(2,1)S(1)}, bf16[192,2048]{1,0:T(8,128)(2,1)S(1)}, u32[]{:S(2)}, u32[]{:S(2)}) collective-permute-start(bf16[192,2048]{1,0:T(8,128)(2,1)S(1)} %copy-done.6), channel_id=1, source_target_pairs={{8,0},{16,8},{24,16},{9,1},{17,9},{25,17},{10,2},{18,10},{26,18},{... | collective-permute-start | bytes 2359304 | tf_op jit(solution)/shard_map/ppermute | solution.py:222
  40.2 8.4 %collective-permute-done.6 = bf16[192,2048]{1,0:T(8,128)(2,1)S(1)} collective-permute-done((bf16[192,2048]{1,0:T(8,128)(2,1)}, bf16[192,2048]{1,0:T(8,128)(2,1)S(1)}, u32[]{:S(2)}, u32[]{:S(2)}) %collective-permute-start.6) | collective-permute-done | bytes 786464 | tf_op jit(solution)/shard_map/ppermute | solution.py:223
  48.6 0.0 collective-permute-done.8
  48.6 1.4 %multiply_convert_fusion = bf16[2,96,2048]{2,1,0:T(8,128)(2,1)S(1)} fusion(bf16[2,96,2048]{2,1,0:T(8,128)(2,1)S(1)} %collective-permute-done.8, bf16[2,96,2048]{2,1,0:T(8,128)(2,1)} %get-tuple-element.18), kind=kLoop, calls=%fused_computation | loop fusion | flops 1966080 | bytes 2359296 | tf_op jit(solution)/shard_map/convert_element_type | solution.py:237
  50.0 0.9 %fusion = (bf16[1,96,2048]{2,1,0:T(8,128)(2,1)}, bf16[1,96,2048]{2,1,0:T(8,128)(2,1)}) fusion(bf16[2,96,2048]{2,1,0:T(8,128)(2,1)S(1)} %multiply_convert_fusion), kind=kLoop, calls=%fused_computation.2 | loop fusion | bytes 1572864 | tf_op jit(solution)/shard_map/slice | solution.py:238
  50.9 9.8 %collective-permute-done.7 = bf16[192,2048]{1,0:T(8,128)(2,1)S(1)} collective-permute-done((bf16[192,2048]{1,0:T(8,128)(2,1)S(1)}, bf16[192,2048]{1,0:T(8,128)(2,1)S(1)}, u32[]{:S(2)}, u32[]{:S(2)}) %collective-permute-start.7) | collective-permute-done | bytes 786464 | tf_op jit(solution)/shard_map/ppermute | solution.py:222
  60.7 0.9 %copy.13 = bf16[1,1,192,2048]{3,2,1,0:T(8,128)(2,1)} copy(bf16[1,1,192,2048]{3,2,1,0:T(8,128)(2,1)S(1)} %bitcast.22) | data formatting | bytes 1572864
  61.6 0.9 %copy.14 = bf16[1,1,192,2048]{3,2,1,0:T(8,128)(2,1)} copy(bf16[1,1,192,2048]{3,2,1,0:T(8,128)(2,1)S(1)} %bitcast.23) | data formatting | bytes 1572864
Async XLA Ops:
  5.9 5.8 %collective-permute-start = (bf16[48,768]{1,0:T(8,128)(2,1)}, bf16[48,768]{1,0:T(8,128)(2,1)S(1)}, u32[]{:S(2)}, u32[]{:S(2)}) collective-permute-start(bf16[48,768]{1,0:T(8,128)(2,1)} %get-tuple-element.13), channel_id=1, source_target_pairs={{0,2},{2,0},{4,6},{6,4},{1,3},{3,1},{5,7},{7,5},{8,10},{10,8},{12,... | collective-permute-start | bytes 221192 | tf_op jit(solution)/shard_map/ppermute | solution.py:34
  8.9 4.6 %collective-permute-start.1 = (bf16[48,768]{1,0:T(8,128)(2,1)}, bf16[48,768]{1,0:T(8,128)(2,1)S(1)}, u32[]{:S(2)}, u32[]{:S(2)}) collective-permute-start(bf16[48,768]{1,0:T(8,128)(2,1)} %get-tuple-element.14), channel_id=1, source_target_pairs={{0,4},{2,6},{4,0},{6,2},{1,5},{3,7},{5,1},{7,3},{8,12},{10,14},{12... | collective-permute-start | bytes 221192 | tf_op jit(solution)/shard_map/ppermute | solution.py:34
  10.5 5.5 %collective-permute-start.2 = (bf16[48,768]{1,0:T(8,128)(2,1)}, bf16[48,768]{1,0:T(8,128)(2,1)S(1)}, u32[]{:S(2)}, u32[]{:S(2)}) collective-permute-start(bf16[48,768]{1,0:T(8,128)(2,1)} %get-tuple-element.15), channel_id=1, source_target_pairs={{0,6},{2,4},{4,2},{6,0},{1,7},{3,5},{5,3},{7,1},{8,14},{10,12},{12... | collective-permute-start | bytes 221192 | tf_op jit(solution)/shard_map/ppermute | solution.py:34
  11.8 4.1 %copy-start.3 = (bf16[48,768]{1,0:T(8,128)(2,1)}, bf16[48,768]{1,0:T(8,128)(2,1)S(1)}, u32[]{:S(2)}) copy-start(bf16[48,768]{1,0:T(8,128)(2,1)S(1)} %collective-permute-done.refs_1_) | copy-start | bytes 221188
  13.5 2.4 %copy-start.4 = (bf16[48,768]{1,0:T(8,128)(2,1)}, bf16[48,768]{1,0:T(8,128)(2,1)S(1)}, u32[]{:S(2)}) copy-start(bf16[48,768]{1,0:T(8,128)(2,1)S(1)} %collective-permute-done.1.refs_2_) | copy-start | bytes 221188
  15.9 0.6 %copy-start.5 = (bf16[48,768]{1,0:T(8,128)(2,1)}, bf16[48,768]{1,0:T(8,128)(2,1)S(1)}, u32[]{:S(2)}) copy-start(bf16[48,768]{1,0:T(8,128)(2,1)S(1)} %collective-permute-done.2.refs_3_) | copy-start | bytes 221188
  18.5 5.6 %collective-permute-start.5 = (bf16[48,768]{1,0:T(8,128)(2,1)}, bf16[48,768]{1,0:T(8,128)(2,1)S(1)}, u32[]{:S(2)}, u32[]{:S(2)}) collective-permute-start(bf16[48,768]{1,0:T(8,128)(2,1)} %middle.1.refs_0_), channel_id=1, source_target_pairs={{0,6},{2,4},{4,2},{6,0},{1,7},{3,5},{5,3},{7,1},{8,14},{10,12},{12... | collective-permute-start | bytes 221192 | tf_op jit(solution)/shard_map/ppermute | solution.py:34
  19.0 5.4 %collective-permute-start.4 = (bf16[48,768]{1,0:T(8,128)(2,1)}, bf16[48,768]{1,0:T(8,128)(2,1)S(1)}, u32[]{:S(2)}, u32[]{:S(2)}) collective-permute-start(bf16[48,768]{1,0:T(8,128)(2,1)} %middle.1.refs_0_), channel_id=1, source_target_pairs={{0,4},{2,6},{4,0},{6,2},{1,5},{3,7},{5,1},{7,3},{8,12},{10,14},{12... | collective-permute-start | bytes 221192 | tf_op jit(solution)/shard_map/ppermute | solution.py:34
  20.5 4.6 %collective-permute-start.3 = (bf16[48,768]{1,0:T(8,128)(2,1)}, bf16[48,768]{1,0:T(8,128)(2,1)S(1)}, u32[]{:S(2)}, u32[]{:S(2)}) collective-permute-start(bf16[48,768]{1,0:T(8,128)(2,1)} %middle.1.refs_0_), channel_id=1, source_target_pairs={{0,2},{2,0},{4,6},{6,4},{1,3},{3,1},{5,7},{7,5},{8,10},{10,8},{12,... | collective-permute-start | bytes 221192 | tf_op jit(solution)/shard_map/ppermute | solution.py:34
  24.1 1.0 %copy-start = (bf16[48,768]{1,0:T(8,128)(2,1)}, bf16[48,768]{1,0:T(8,128)(2,1)S(1)}, u32[]{:S(2)}) copy-start(bf16[48,768]{1,0:T(8,128)(2,1)S(1)} %collective-permute-done.5.refs_3_) | copy-start | bytes 221188
  24.3 0.8 %copy-start.1 = (bf16[48,768]{1,0:T(8,128)(2,1)}, bf16[48,768]{1,0:T(8,128)(2,1)S(1)}, u32[]{:S(2)}) copy-start(bf16[48,768]{1,0:T(8,128)(2,1)S(1)} %collective-permute-done.4.refs_2_) | copy-start | bytes 221188
  25.1 0.6 %copy-start.2 = (bf16[48,768]{1,0:T(8,128)(2,1)}, bf16[48,768]{1,0:T(8,128)(2,1)S(1)}, u32[]{:S(2)}) copy-start(bf16[48,768]{1,0:T(8,128)(2,1)S(1)} %collective-permute-done.3.refs_1_) | copy-start | bytes 221188
  30.5 8.4 %copy-start.6 = (bf16[192,2048]{1,0:T(8,128)(2,1)S(1)}, bf16[192,2048]{1,0:T(8,128)(2,1)}, u32[]{:S(2)}) copy-start(bf16[192,2048]{1,0:T(8,128)(2,1)} %get-tuple-element.17) | copy-start | bytes 2359300
  30.5 18.1 %collective-permute-start.6 = (bf16[192,2048]{1,0:T(8,128)(2,1)}, bf16[192,2048]{1,0:T(8,128)(2,1)S(1)}, u32[]{:S(2)}, u32[]{:S(2)}) collective-permute-start(bf16[192,2048]{1,0:T(8,128)(2,1)} %get-tuple-element.16), channel_id=1, source_target_pairs={{0,8},{8,16},{16,24},{1,9},{9,17},{17,25},{2,10},{10,18},{18,26},{... | collective-permute-start | bytes 2359304 | tf_op jit(solution)/shard_map/ppermute | solution.py:223
  38.9 9.7 %collective-permute-start.8 = (bf16[2,96,2048]{2,1,0:T(8,128)(2,1)}, bf16[2,96,2048]{2,1,0:T(8,128)(2,1)S(1)}, u32[]{:S(2)}, u32[]{:S(2)}) collective-permute-start(bf16[2,96,2048]{2,1,0:T(8,128)(2,1)} %get-tuple-element.19), channel_id=1, source_target_pairs={{0,1},{1,0},{2,3},{3,2},{4,5},{5,4},{6,7},{7,6},{8,9},{9,8},{10,11... | collective-permute-start | bytes 2359304 | tf_op jit(solution)/shard_map/ppermute | solution.py:34
  38.9 21.8 %collective-permute-start.7 = (bf16[192,2048]{1,0:T(8,128)(2,1)S(1)}, bf16[192,2048]{1,0:T(8,128)(2,1)S(1)}, u32[]{:S(2)}, u32[]{:S(2)}) collective-permute-start(bf16[192,2048]{1,0:T(8,128)(2,1)S(1)} %copy-done.6), channel_id=1, source_target_pairs={{8,0},{16,8},{24,16},{9,1},{17,9},{25,17},{10,2},{18,10},{26,18},{... | collective-permute-start | bytes 2359304 | tf_op jit(solution)/shard_map/ppermute | solution.py:222

commit v2 on v1

--- a/solution.py
+++ b/solution.py
@@ -9,6 +9,7 @@
 
 EPSILON = 1e-05
 LANES = 128
+BLOCK = 512
 F32 = jnp.float32
 BF16 = jnp.bfloat16
 
@@ -32,6 +33,10 @@
 def send_step(cells, axis, step):
     count = lax.axis_size(axis)
     return lax.ppermute(cells, axis, [(i, partner(i, step, count)) for i in range(count)])
+
+
+def near(cells):
+    return pltpu.with_memory_space_constraint(cells, pltpu.VMEM)
 
 
 def contract_last(left_side, right_side):
@@ -64,7 +69,7 @@
     return row < limit
 
 
-def partials_body(unit_count, slot, share_count, place_ref, fwd_ref, saved_ref, grad_ref, gain_ref, down_ref, up_ref, *refs):
+def partials_body(unit_count, slot, share_count, fwd_ref, saved_ref, grad_ref, gain_ref, down_ref, up_ref, *refs):
     outs = refs[:share_count]
     acc_ref, squares_ref = refs[share_count:]
     step = pl.program_id(0)
@@ -95,17 +100,17 @@
             acc_ref[:, lo : lo + slot] = place_pair(acc_ref[:, lo : lo + slot], unit_count, split_pair(total))
         share_rows = outs[0].shape[0]
         for k, out in enumerate(outs):
-            first = pl.multiple_of(partner(place_ref[0], k, share_count) * share_rows, share_rows)
+            first = pl.multiple_of(partner(lax.axis_index("tensor"), k, share_count) * share_rows, share_rows)
             out[...] = acc_ref[pl.ds(first, share_rows), :].astype(BF16)
 
 
-def middle_body(unit_count, slot, full_width, seq_rows, place_ref, lengths_ref, *refs):
+def middle_body(unit_count, slot, full_width, seq_rows, lengths_ref, *refs):
     parts, out = refs[:-1], refs[-1]
     total = parts[0][...].astype(F32)
     for part in parts[1:]:
         total += part[...].astype(F32)
     share_rows = total.shape[0]
-    keep = keep_mask(place_ref[0] * share_rows, (share_rows, slot), seq_rows, lengths_ref)
+    keep = keep_mask(lax.axis_index("tensor") * share_rows, (share_rows, slot), seq_rows, lengths_ref)
     fwd, saved, slope = (total[:, i * slot : (i + 1) * slot] for i in range(3))
     fwd_scale = lax.rsqrt(take_pair(fwd, unit_count) / full_width + EPSILON)
     saved_scale = lax.rsqrt(take_pair(saved, unit_count) / full_width + EPSILON)
@@ -121,33 +126,35 @@
     out[:, 2 * slot :] = place_pair(back * saved_scale, unit_count, split_pair(bend)).astype(BF16)
 
 
-def join_shares(place_ref, shares, whole_ref):
+def join_shares(shares, whole_ref):
     share_rows = shares[0].shape[0]
     for k, share in enumerate(shares):
-        first = source(place_ref[0], k, len(shares)) * share_rows
+        first = source(lax.axis_index("tensor"), k, len(shares)) * share_rows
         whole_ref[pl.ds(pl.multiple_of(first, share_rows), share_rows), :] = share[...]
 
 
-def edges_body(unit_count, slot, share_count, seq_rows, place_ref, lengths_ref, *refs):
+def edges_body(unit_count, slot, share_count, seq_rows, lengths_ref, *refs):
     shares = refs[:share_count]
     fwd_ref, saved_ref, grad_ref, gain_ref, down_ref, up_ref, out_fwd, out_grad, whole_ref = refs[share_count:]
 
     @pl.when(pl.program_id(0) == 0)
     def _():
-        join_shares(place_ref, shares, whole_ref)
-
+        join_shares(shares, whole_ref)
+
+    block = grad_ref.shape[1]
+    here = pl.ds(pl.multiple_of(pl.program_id(0) * block, block), block)
     keep = keep_mask(0, grad_ref.shape, seq_rows, lengths_ref)
     back = whole_ref[:, 2 * slot : 2 * slot + unit_count]
     bend = take_pair(whole_ref[:, 2 * slot :].astype(F32), unit_count)
     weighted = jnp.dot(back, down_ref[...], preferred_element_type=F32) * gain_ref[...].astype(F32)
     kept = jnp.where(keep, grad_ref[...].astype(F32), 0.0)
-    out_grad[...] = (kept + weighted - saved_ref[...].astype(F32) * bend).astype(BF16)
+    out_grad[:, here] = (kept + weighted - saved_ref[...].astype(F32) * bend).astype(BF16)
     act = whole_ref[:, 0:unit_count]
     lifted = jnp.dot(act, up_ref[...], preferred_element_type=F32)
-    out_fwd[...] = (fwd_ref[...].astype(F32) + lifted).astype(BF16)
-
-
-def grads_body(unit_count, slot, share_count, place_ref, *refs):
+    out_fwd[:, here] = (fwd_ref[...].astype(F32) + lifted).astype(BF16)
+
+
+def grads_body(unit_count, slot, share_count, *refs):
     shares = refs[:share_count]
     saved_ref, grad_ref, gain_ref = refs[share_count : share_count + 3]
     outs = refs[share_count + 3 : -2]
@@ -155,7 +162,7 @@
 
     @pl.when(pl.program_id(0) == 0)
     def _():
-        join_shares(place_ref, shares, whole_ref)
+        join_shares(shares, whole_ref)
 
     back = whole_ref[:, 2 * slot : 2 * slot + unit_count]
     act = whole_ref[:, slot : slot + unit_count]
@@ -164,9 +171,18 @@
     group_count = len(outs)
     group_rows = unit_count // group_count
     for k, out in enumerate(outs):
-        first = partner(place_ref[1], k, group_count) * group_rows
+        first = partner(lax.axis_index("dp"), k, group_count) * group_rows
         for which in range(2):
             out[which] = hold_ref[which, pl.ds(pl.multiple_of(first, group_rows), group_rows), :].astype(BF16)
+
+
+def land_body(first_ref, second_ref, first_out, second_out, first_sem, second_sem):
+    first = pltpu.make_async_copy(first_ref, first_out, first_sem)
+    second = pltpu.make_async_copy(second_ref, second_out, second_sem)
+    first.start()
+    second.start()
+    first.wait()
+    second.wait()
 
 
 def shards(forward_rows, saved_rows, output_grad, lengths, norm_gain, down_map, up_map):
@@ -183,58 +199,67 @@
     full_width = width * share_count
     slot = round_up(unit_count + 2, LANES)
     packed = 3 * slot
-    place = jnp.stack([lax.axis_index("tensor"), lax.axis_index("dp")]).astype(jnp.int32)
-    block = min(width, 512)
+    block = min(width, BLOCK)
     steps = width // block
     smem = pl.BlockSpec(memory_space=pltpu.SMEM)
     cols = lambda n: pl.BlockSpec((n, block), lambda j: (0, j))
-    whole = pl.BlockSpec((share_rows, packed), lambda j: (0, 0))
-    share_type = jax.ShapeDtypeStruct((share_rows, packed), BF16)
+    whole = pl.BlockSpec(memory_space=pltpu.VMEM)
+    share_type = pltpu.VMEM((share_rows, packed), BF16)
 
     parts = pl.pallas_call(
         functools.partial(partials_body, unit_count, slot, share_count),
         grid=(steps,),
-        in_specs=[smem, cols(row_count), cols(row_count), cols(row_count), cols(1), cols(unit_count), cols(unit_count)],
+        in_specs=[cols(row_count), cols(row_count), cols(row_count), cols(1), cols(unit_count), cols(unit_count)],
         out_specs=[whole] * share_count,
         out_shape=[share_type] * share_count,
         scratch_shapes=[pltpu.VMEM((row_count, packed), F32), pltpu.VMEM((2, row_count, LANES), F32)],
         name="partials",
-    )(place, fwd, saved, grad, norm_gain, down, up)
-    got = [parts[0]] + [send_step(parts[k], "tensor", k) for k in range(1, share_count)]
+    )(fwd, saved, grad, norm_gain, down, up)
+    got = [near(parts[0])] + [near(send_step(parts[k], "tensor", k)) for k in range(1, share_count)]
     mine = pl.pallas_call(
         functools.partial(middle_body, unit_count, slot, full_width, seq_rows),
-        in_specs=[smem, smem] + [pl.BlockSpec(memory_space=pltpu.VMEM)] * share_count,
+        in_specs=[smem] + [pl.BlockSpec(memory_space=pltpu.VMEM)] * share_count,
         out_specs=pl.BlockSpec(memory_space=pltpu.VMEM),
         out_shape=share_type,
         name="middle",
-    )(place, seq_lengths, *got)
-    shares = [mine] + [send_step(mine, "tensor", k) for k in range(1, share_count)]
+    )(seq_lengths, *got)
+    shares = [near(mine)] + [near(send_step(mine, "tensor", k)) for k in range(1, share_count)]
     out_fwd, out_grad = pl.pallas_call(
         functools.partial(edges_body, unit_count, slot, share_count, seq_rows),
         grid=(steps,),
-        in_specs=[smem, smem] + [whole] * share_count
+        in_specs=[smem] + [whole] * share_count
         + [cols(row_count), cols(row_count), cols(row_count), cols(1), cols(unit_count), cols(unit_count)],
-        out_specs=[cols(row_count)] * 2,
-        out_shape=[jax.ShapeDtypeStruct((row_count, width), BF16)] * 2,
+        out_specs=[whole] * 2,
+        out_shape=[pltpu.VMEM((row_count, width), BF16)] * 2,
         scratch_shapes=[pltpu.VMEM((row_count, packed), BF16)],
         name="edges",
-    )(place, seq_lengths, *shares, fwd, saved, grad, norm_gain, down, up)
-    next_grads = lax.ppermute(out_grad, "section", [(i + 1, i) for i in range(section_count - 1)])
-    next_inputs = lax.ppermute(out_fwd, "section", [(i, i + 1) for i in range(section_count - 1)])
+    )(seq_lengths, *shares, fwd, saved, grad, norm_gain, down, up)
+    next_grads = lax.ppermute(near(out_grad), "section", [(i + 1, i) for i in range(section_count - 1)])
+    next_inputs = lax.ppermute(near(out_fwd), "section", [(i, i + 1) for i in range(section_count - 1)])
     group_rows = unit_count // group_count
-    halves = pl.pallas_call(
+    sum_maps = pl.pallas_call(
         functools.partial(grads_body, unit_count, slot, share_count),
         grid=(steps,),
-        in_specs=[smem] + [whole] * share_count + [cols(row_count), cols(row_count), cols(1)],
+        in_specs=[whole] * share_count + [cols(row_count), cols(row_count), cols(1)],
         out_specs=[pl.BlockSpec((2, group_rows, block), lambda j: (0, 0, j))] * group_count,
         out_shape=[jax.ShapeDtypeStruct((2, group_rows, width), BF16)] * group_count,
         scratch_shapes=[pltpu.VMEM((row_count, packed), BF16), pltpu.VMEM((2, unit_count, block), F32)],
+        cost_estimate=pl.CostEstimate(flops=40 * row_count * unit_count * width, bytes_accessed=6 * row_count * width, transcendentals=0),
         name="grads",
-    )(place, *shares, saved, grad, norm_gain)
+    )
+    halves = sum_maps(*shares, saved, grad, norm_gain)
     total = halves[0].astype(F32)
     for k in range(1, group_count):
         total += send_step(halves[k], "dp", k).astype(F32)
     mean = (total * (1.0 / group_count)).astype(BF16)
+    next_inputs, next_grads = pl.pallas_call(
+        land_body,
+        in_specs=[whole] * 2,
+        out_specs=[pl.BlockSpec(memory_space=pl.ANY)] * 2,
+        out_shape=[jax.ShapeDtypeStruct((row_count, width), BF16)] * 2,
+        scratch_shapes=[pltpu.SemaphoreType.DMA] * 2,
+        name="land",
+    )(near(next_inputs), near(next_grads))
     return (next_inputs[None, None], next_grads[None, None], mean[0:1], mean[1:2])
 
 

time: 62.9 us -> 56.3 us (0.90)
  local copies, waits for them, and re-layouts: 3.97 us -> 0.93 us
  Pallas kernels: 16.1 us -> 14 us
  waiting for transfers between devices: 26.7 us -> 25.8 us
    unnamed x16 -> x0, local copies, waits for them, and re-layouts: 3.04 us -> none
    pallas_call x1, Pallas kernels: 4.76 us -> 3.62 us  [shards(): pl.pallas_call(functools.partial(edges_body, unit_count, slot, share_coun...]
    pallas_call x1, Pallas kernels: 1.97 us -> 1 us  [shards(): pl.pallas_call(functools.partial(middle_body, unit_count, slot, full_widt...]
    pallas_call x1 -> x2, Pallas kernels: 4.68 us -> 5.42 us  [the longest x1 4.26 us: shards(): halves = sum_maps(*shares, saved, grad, norm_gain)]
    pallas_call x1, Pallas kernels: 4.65 us -> 3.96 us  [shards(): pl.pallas_call(functools.partial(partials_body, unit_count, slot, share_c...]
    another operation x1 -> x0, other arithmetic: 0.66 us -> none  [shards(): jnp.stack([lax.axis_index('tensor'), lax.axis_index('dp')])]
  transfers between devices with their start and end apart: 9 -> 9, of which waited for: 8 -> 8; matrix products, arithmetic and copies ran while one was open for 4% -> 5% of each run, Pallas kernels for 7% -> 6%
where the time goes in v2:
time: 56.3 us; the launch traced here: 55.9 us
  waiting for transfers between devices  25.8 us (46%)
  Pallas kernels  14 us (25%)
  starting transfers between devices  12.9 us (23%)
  other arithmetic  1.65 us (3%)
  local copies, waits for them, and re-layouts  0.93 us (2%)
  between operations  0.69 us (1%)
    ppermute x1, waiting for transfers between devices, shards(): lax.ppermute(near(out_fwd), 'section', [(i, i + 1) for i in range(section...  13.5 us
    ppermute x7, starting transfers between devices, send_step(): lax.ppermute(cells, axis, [(i, partner(i, step, count)) for i in range(co...  8.13 us
    ppermute x7, waiting for transfers between devices, send_step(): lax.ppermute(cells, axis, [(i, partner(i, step, count)) for i in range(co...  8.09 us
    pallas_call x1, Pallas kernels, shards(): halves = sum_maps(*shares, saved, grad, norm_gain)  4.26 us
    ppermute x1, waiting for transfers between devices, shards(): lax.ppermute(near(out_grad), 'section', [(i + 1, i) for i in range(sectio...  4.16 us
    pallas_call x1, Pallas kernels, shards(): pl.pallas_call(functools.partial(partials_body, unit_count, slot, share_c...  3.96 us
    pallas_call x1, Pallas kernels, shards(): pl.pallas_call(functools.partial(edges_body, unit_count, slot, share_coun...  3.62 us
    ppermute x1, starting transfers between devices, shards(): lax.ppermute(near(out_fwd), 'section', [(i, i + 1) for i in range(section...  3.48 us
  transfers between devices with their start and end apart: 9, of which 8 were waited for; matrix products, arithmetic and copies ran while one was open for 5% of the time, Pallas kernels for 6%

profile of v2, /device:TPU:0, one launch (start us, length us, event | category | flops | bytes accessed | tf_op | source)
XLA Modules:
  0.0 55.9 jit_solution(15272403680762829199)
XLA Ops:
  0.6 4.0 %partials.1 = (bf16[48,768]{1,0:T(8,128)(2,1)S(1)}, bf16[48,768]{1,0:T(8,128)(2,1)S(1)}, bf16[48,768]{1,0:T(8,128)(2,1)S(1)}, bf16[48,768]{1,0:T(8,128)(2,1)S(1)}) custom-call(bf16[192,2048]{1,0:T(8,128)(2,1)} %bitcast.8, bf16[192,2048]{1,0:T(8,128)(2,1)} %bitcast.10, bf16[192,2048]{1,0:T(8,128)(2,1)} %bitcast.13, bf16[1,2048]{1,0:T(2,128)(2,1)} %refs_6_.1, ...), custom_call_target="tpu_custom_call" | custom-call | tf_op jit(solution)/shard_map/partials/pallas_call | solution.py:209
  4.6 3.0 %collective-permute-start = (bf16[48,768]{1,0:T(8,128)(2,1)S(1)}, bf16[48,768]{1,0:T(8,128)(2,1)S(1)}, u32[]{:S(2)}, u32[]{:S(2)}) collective-permute-start(bf16[48,768]{1,0:T(8,128)(2,1)S(1)} %get-tuple-element.15), channel_id=1, source_target_pairs={{0,2},{2,0},{4,6},{6,4},{1,3},{3,1},{5,7},{7,5},{8,10},{10,8},{12,... | collective-permute-start | bytes 221192 | tf_op jit(solution)/shard_map/ppermute | solution.py:35
  7.6 1.5 %collective-permute-start.1 = (bf16[48,768]{1,0:T(8,128)(2,1)S(1)}, bf16[48,768]{1,0:T(8,128)(2,1)S(1)}, u32[]{:S(2)}, u32[]{:S(2)}) collective-permute-start(bf16[48,768]{1,0:T(8,128)(2,1)S(1)} %get-tuple-element.16), channel_id=1, source_target_pairs={{0,4},{2,6},{4,0},{6,2},{1,5},{3,7},{5,1},{7,3},{8,12},{10,14},{12... | collective-permute-start | bytes 221192 | tf_op jit(solution)/shard_map/ppermute | solution.py:35
  9.1 0.0 collective-permute-start.2
  9.2 1.0 %collective-permute-done.refs_1_ = bf16[48,768]{1,0:T(8,128)(2,1)S(1)} collective-permute-done((bf16[48,768]{1,0:T(8,128)(2,1)S(1)}, bf16[48,768]{1,0:T(8,128)(2,1)S(1)}, u32[]{:S(2)}, u32[]{:S(2)}) %collective-permute-start) | collective-permute-done | bytes 73760 | tf_op jit(solution)/shard_map/ppermute | solution.py:35
  10.2 1.8 %collective-permute-done.1.refs_2_ = bf16[48,768]{1,0:T(8,128)(2,1)S(1)} collective-permute-done((bf16[48,768]{1,0:T(8,128)(2,1)S(1)}, bf16[48,768]{1,0:T(8,128)(2,1)S(1)}, u32[]{:S(2)}, u32[]{:S(2)}) %collective-permute-start.1) | collective-permute-done | bytes 73760 | tf_op jit(solution)/shard_map/ppermute | solution.py:35
  12.0 2.4 %collective-permute-done.2.refs_3_ = bf16[48,768]{1,0:T(8,128)(2,1)S(1)} collective-permute-done((bf16[48,768]{1,0:T(8,128)(2,1)S(1)}, bf16[48,768]{1,0:T(8,128)(2,1)S(1)}, u32[]{:S(2)}, u32[]{:S(2)}) %collective-permute-start.2) | collective-permute-done | bytes 73760 | tf_op jit(solution)/shard_map/ppermute | solution.py:35
  14.4 1.0 %middle.1.refs_0_ = bf16[48,768]{1,0:T(8,128)(2,1)S(1)} custom-call(s32[2]{0:T(128)} %bitcast.20, bf16[48,768]{1,0:T(8,128)(2,1)S(1)} %get-tuple-element.14.refs_0_, bf16[48,768]{1,0:T(8,128)(2,1)S(1)} %collective-permute-done.refs_1_, bf16[48,768]{1,0:T(8,128)(2,1)S(1)} %collective-permute-done.1.refs_2_, bf16[48,768]{1,0:T(8,128)(2,1)S(1)} %collective-permute-done.2.refs_3_), custom_call_target="tpu_custom_call" | custom-call | tf_op jit(solution)/shard_map/middle/pallas_call | solution.py:219
  15.4 0.5 collective-permute-start.5
  15.9 1.6 %collective-permute-start.4 = (bf16[48,768]{1,0:T(8,128)(2,1)S(1)}, bf16[48,768]{1,0:T(8,128)(2,1)S(1)}, u32[]{:S(2)}, u32[]{:S(2)}) collective-permute-start(bf16[48,768]{1,0:T(8,128)(2,1)S(1)} %middle.1.refs_0_), channel_id=1, source_target_pairs={{0,4},{2,6},{4,0},{6,2},{1,5},{3,7},{5,1},{7,3},{8,12},{10,14},{12... | collective-permute-start | bytes 221192 | tf_op jit(solution)/shard_map/ppermute | solution.py:35
  17.5 1.5 %collective-permute-start.3 = (bf16[48,768]{1,0:T(8,128)(2,1)S(1)}, bf16[48,768]{1,0:T(8,128)(2,1)S(1)}, u32[]{:S(2)}, u32[]{:S(2)}) collective-permute-start(bf16[48,768]{1,0:T(8,128)(2,1)S(1)} %middle.1.refs_0_), channel_id=1, source_target_pairs={{0,2},{2,0},{4,6},{6,4},{1,3},{3,1},{5,7},{7,5},{8,10},{10,8},{12,... | collective-permute-start | bytes 221192 | tf_op jit(solution)/shard_map/ppermute | solution.py:35
  19.0 1.9 %collective-permute-done.5.refs_3_ = bf16[48,768]{1,0:T(8,128)(2,1)S(1)} collective-permute-done((bf16[48,768]{1,0:T(8,128)(2,1)S(1)}, bf16[48,768]{1,0:T(8,128)(2,1)S(1)}, u32[]{:S(2)}, u32[]{:S(2)}) %collective-permute-start.5) | collective-permute-done | bytes 73760 | tf_op jit(solution)/shard_map/ppermute | solution.py:35
  20.8 0.2 collective-permute-done.4.refs_2_
  21.0 0.8 %collective-permute-done.3.refs_1_ = bf16[48,768]{1,0:T(8,128)(2,1)S(1)} collective-permute-done((bf16[48,768]{1,0:T(8,128)(2,1)S(1)}, bf16[48,768]{1,0:T(8,128)(2,1)S(1)}, u32[]{:S(2)}, u32[]{:S(2)}) %collective-permute-start.3) | collective-permute-done | bytes 73760 | tf_op jit(solution)/shard_map/ppermute | solution.py:35
  21.8 4.3 %grads.1 = (bf16[2,96,2048]{2,1,0:T(8,128)(2,1)}, bf16[2,96,2048]{2,1,0:T(8,128)(2,1)}) custom-call(bf16[48,768]{1,0:T(8,128)(2,1)S(1)} %middle.1.refs_0_, bf16[48,768]{1,0:T(8,128)(2,1)S(1)} %collective-permute-done.3.refs_1_, bf16[48,768]{1,0:T(8,128)(2,1)S(1)} %collective-permute-done.4.refs_2_, bf16[48,768]{1,0:T(8,128)(2,1)S(1)} %collective-permute-done.5.refs_3_, ...), custom_call_target="tpu_custom_call" | custom-call | flops 3019898880 | bytes 2359296 | tf_op jit(solution)/shard_map/grads/pallas_call | solution.py:250
  26.1 0.0 collective-permute-start.8
  26.1 3.6 %edges.1 = (bf16[192,2048]{1,0:T(8,128)(2,1)S(1)}, bf16[192,2048]{1,0:T(8,128)(2,1)S(1)}) custom-call(s32[2]{0:T(128)} %bitcast.21, bf16[48,768]{1,0:T(8,128)(2,1)S(1)} %middle.1.refs_0_, bf16[48,768]{1,0:T(8,128)(2,1)S(1)} %collective-permute-done.3.refs_1_, bf16[48,768]{1,0:T(8,128)(2,1)S(1)} %collective-permute-done.4.refs_2_, ...), custom_call_target="tpu_custom_call" | custom-call | tf_op jit(solution)/shard_map/edges/pallas_call | solution.py:227
  29.7 3.5 %collective-permute-start.6 = (bf16[192,2048]{1,0:T(8,128)(2,1)S(1)}, bf16[192,2048]{1,0:T(8,128)(2,1)S(1)}, u32[]{:S(2)}, u32[]{:S(2)}) collective-permute-start(bf16[192,2048]{1,0:T(8,128)(2,1)S(1)} %get-tuple-element.18), channel_id=1, source_target_pairs={{0,8},{8,16},{16,24},{1,9},{9,17},{17,25},{2,10},{10,18},{18,26},{... | collective-permute-start | bytes 2359304 | tf_op jit(solution)/shard_map/ppermute | solution.py:238
  33.2 1.3 %collective-permute-start.7 = (bf16[192,2048]{1,0:T(8,128)(2,1)S(1)}, bf16[192,2048]{1,0:T(8,128)(2,1)S(1)}, u32[]{:S(2)}, u32[]{:S(2)}) collective-permute-start(bf16[192,2048]{1,0:T(8,128)(2,1)S(1)} %get-tuple-element.19), channel_id=1, source_target_pairs={{8,0},{16,8},{24,16},{9,1},{17,9},{25,17},{10,2},{18,10},{26,18},{... | collective-permute-start | bytes 2359304 | tf_op jit(solution)/shard_map/ppermute | solution.py:237
  34.5 0.0 collective-permute-done.8
  34.5 1.7 %multiply_convert_fusion = bf16[2,96,2048]{2,1,0:T(8,128)(2,1)S(1)} fusion(bf16[2,96,2048]{2,1,0:T(8,128)(2,1)} %collective-permute-done.8, bf16[2,96,2048]{2,1,0:T(8,128)(2,1)} %get-tuple-element.22), kind=kLoop, calls=%fused_computation | loop fusion | flops 1966080 | bytes 2359296 | tf_op jit(solution)/shard_map/convert_element_type | solution.py:254
  36.2 0.9 %fusion = (bf16[1,96,2048]{2,1,0:T(8,128)(2,1)}, bf16[1,96,2048]{2,1,0:T(8,128)(2,1)}) fusion(bf16[2,96,2048]{2,1,0:T(8,128)(2,1)S(1)} %multiply_convert_fusion), kind=kLoop, calls=%fused_computation.1 | loop fusion | bytes 1572864 | tf_op jit(solution)/shard_map/slice | solution.py:263
  37.1 13.5 %collective-permute-done.6.first_ref = bf16[192,2048]{1,0:T(8,128)(2,1)S(1)} collective-permute-done((bf16[192,2048]{1,0:T(8,128)(2,1)S(1)}, bf16[192,2048]{1,0:T(8,128)(2,1)S(1)}, u32[]{:S(2)}, u32[]{:S(2)}) %collective-permute-start.6) | collective-permute-done | bytes 786464 | tf_op jit(solution)/shard_map/ppermute | solution.py:238
  50.6 4.2 %collective-permute-done.7.second_ref = bf16[192,2048]{1,0:T(8,128)(2,1)S(1)} collective-permute-done((bf16[192,2048]{1,0:T(8,128)(2,1)S(1)}, bf16[192,2048]{1,0:T(8,128)(2,1)S(1)}, u32[]{:S(2)}, u32[]{:S(2)}) %collective-permute-start.7) | collective-permute-done | bytes 786464 | tf_op jit(solution)/shard_map/ppermute | solution.py:237
  54.7 1.2 %land.1 = (bf16[192,2048]{1,0:T(8,128)(2,1)}, bf16[192,2048]{1,0:T(8,128)(2,1)}) custom-call(bf16[192,2048]{1,0:T(8,128)(2,1)S(1)} %collective-permute-done.6.first_ref, bf16[192,2048]{1,0:T(8,128)(2,1)S(1)} %collective-permute-done.7.second_ref), custom_call_target="tpu_custom_call" | custom-call | tf_op jit(solution)/shard_map/land/pallas_call | solution.py:255
Async XLA Ops:
  4.6 5.6 %collective-permute-start = (bf16[48,768]{1,0:T(8,128)(2,1)S(1)}, bf16[48,768]{1,0:T(8,128)(2,1)S(1)}, u32[]{:S(2)}, u32[]{:S(2)}) collective-permute-start(bf16[48,768]{1,0:T(8,128)(2,1)S(1)} %get-tuple-element.15), channel_id=1, source_target_pairs={{0,2},{2,0},{4,6},{6,4},{1,3},{3,1},{5,7},{7,5},{8,10},{10,8},{12,... | collective-permute-start | bytes 221192 | tf_op jit(solution)/shard_map/ppermute | solution.py:35
  7.6 4.4 %collective-permute-start.1 = (bf16[48,768]{1,0:T(8,128)(2,1)S(1)}, bf16[48,768]{1,0:T(8,128)(2,1)S(1)}, u32[]{:S(2)}, u32[]{:S(2)}) collective-permute-start(bf16[48,768]{1,0:T(8,128)(2,1)S(1)} %get-tuple-element.16), channel_id=1, source_target_pairs={{0,4},{2,6},{4,0},{6,2},{1,5},{3,7},{5,1},{7,3},{8,12},{10,14},{12... | collective-permute-start | bytes 221192 | tf_op jit(solution)/shard_map/ppermute | solution.py:35
  9.1 5.3 %collective-permute-start.2 = (bf16[48,768]{1,0:T(8,128)(2,1)S(1)}, bf16[48,768]{1,0:T(8,128)(2,1)S(1)}, u32[]{:S(2)}, u32[]{:S(2)}) collective-permute-start(bf16[48,768]{1,0:T(8,128)(2,1)S(1)} %get-tuple-element.17), channel_id=1, source_target_pairs={{0,6},{2,4},{4,2},{6,0},{1,7},{3,5},{5,3},{7,1},{8,14},{10,12},{12... | collective-permute-start | bytes 221192 | tf_op jit(solution)/shard_map/ppermute | solution.py:35
  15.4 5.4 %collective-permute-start.5 = (bf16[48,768]{1,0:T(8,128)(2,1)S(1)}, bf16[48,768]{1,0:T(8,128)(2,1)S(1)}, u32[]{:S(2)}, u32[]{:S(2)}) collective-permute-start(bf16[48,768]{1,0:T(8,128)(2,1)S(1)} %middle.1.refs_0_), channel_id=1, source_target_pairs={{0,6},{2,4},{4,2},{6,0},{1,7},{3,5},{5,3},{7,1},{8,14},{10,12},{12... | collective-permute-start | bytes 221192 | tf_op jit(solution)/shard_map/ppermute | solution.py:35
  15.9 5.1 %collective-permute-start.4 = (bf16[48,768]{1,0:T(8,128)(2,1)S(1)}, bf16[48,768]{1,0:T(8,128)(2,1)S(1)}, u32[]{:S(2)}, u32[]{:S(2)}) collective-permute-start(bf16[48,768]{1,0:T(8,128)(2,1)S(1)} %middle.1.refs_0_), channel_id=1, source_target_pairs={{0,4},{2,6},{4,0},{6,2},{1,5},{3,7},{5,1},{7,3},{8,12},{10,14},{12... | collective-permute-start | bytes 221192 | tf_op jit(solution)/shard_map/ppermute | solution.py:35
  17.5 4.4 %collective-permute-start.3 = (bf16[48,768]{1,0:T(8,128)(2,1)S(1)}, bf16[48,768]{1,0:T(8,128)(2,1)S(1)}, u32[]{:S(2)}, u32[]{:S(2)}) collective-permute-start(bf16[48,768]{1,0:T(8,128)(2,1)S(1)} %middle.1.refs_0_), channel_id=1, source_target_pairs={{0,2},{2,0},{4,6},{6,4},{1,3},{3,1},{5,7},{7,5},{8,10},{10,8},{12,... | collective-permute-start | bytes 221192 | tf_op jit(solution)/shard_map/ppermute | solution.py:35
  26.1 8.4 %collective-permute-start.8 = (bf16[2,96,2048]{2,1,0:T(8,128)(2,1)}, bf16[2,96,2048]{2,1,0:T(8,128)(2,1)}, u32[]{:S(2)}, u32[]{:S(2)}) collective-permute-start(bf16[2,96,2048]{2,1,0:T(8,128)(2,1)} %get-tuple-element.23), channel_id=1, source_target_pairs={{0,1},{1,0},{2,3},{3,2},{4,5},{5,4},{6,7},{7,6},{8,9},{9,8},{10,11... | collective-permute-start | bytes 2359304 | tf_op jit(solution)/shard_map/ppermute | solution.py:35
  29.7 20.9 %collective-permute-start.6 = (bf16[192,2048]{1,0:T(8,128)(2,1)S(1)}, bf16[192,2048]{1,0:T(8,128)(2,1)S(1)}, u32[]{:S(2)}, u32[]{:S(2)}) collective-permute-start(bf16[192,2048]{1,0:T(8,128)(2,1)S(1)} %get-tuple-element.18), channel_id=1, source_target_pairs={{0,8},{8,16},{16,24},{1,9},{9,17},{17,25},{2,10},{10,18},{18,26},{... | collective-permute-start | bytes 2359304 | tf_op jit(solution)/shard_map/ppermute | solution.py:238
  33.2 21.6 %collective-permute-start.7 = (bf16[192,2048]{1,0:T(8,128)(2,1)S(1)}, bf16[192,2048]{1,0:T(8,128)(2,1)S(1)}, u32[]{:S(2)}, u32[]{:S(2)}) collective-permute-start(bf16[192,2048]{1,0:T(8,128)(2,1)S(1)} %get-tuple-element.19), channel_id=1, source_target_pairs={{8,0},{16,8},{24,16},{9,1},{17,9},{25,17},{10,2},{18,10},{26,18},{... | collective-permute-start | bytes 2359304 | tf_op jit(solution)/shard_map/ppermute | solution.py:237

commit v3 on v2

--- a/solution.py
+++ b/solution.py
@@ -10,6 +10,7 @@
 EPSILON = 1e-05
 LANES = 128
 BLOCK = 512
+CHUNKS = 2
 F32 = jnp.float32
 BF16 = jnp.bfloat16
 
@@ -79,12 +80,11 @@
         acc_ref[...] = jnp.zeros_like(acc_ref)
         squares_ref[...] = jnp.zeros_like(squares_ref)
 
-    gain = gain_ref[...].astype(F32)
-    down = down_ref[...]
+    down = (down_ref[...].astype(F32) * gain_ref[...].astype(F32)).astype(BF16)
     for which, rows_ref in enumerate((fwd_ref, saved_ref)):
         values = rows_ref[...].astype(F32)
         lo = which * slot
-        acc_ref[:, lo : lo + unit_count] += contract_last((values * gain).astype(BF16), down)
+        acc_ref[:, lo : lo + unit_count] += contract_last(rows_ref[...], down)
         total = squares_ref[which]
         for c in range(0, values.shape[1], LANES):
             part = values[:, c : c + LANES]
@@ -170,15 +170,30 @@
     hold_ref[1] = contract_rows(act, grad_ref[...])
     group_count = len(outs)
     group_rows = unit_count // group_count
+    block = grad_ref.shape[1]
+    here = pl.ds(pl.multiple_of(pl.program_id(0) * block, block), block)
     for k, out in enumerate(outs):
         first = partner(lax.axis_index("dp"), k, group_count) * group_rows
         for which in range(2):
-            out[which] = hold_ref[which, pl.ds(pl.multiple_of(first, group_rows), group_rows), :].astype(BF16)
-
-
-def land_body(first_ref, second_ref, first_out, second_out, first_sem, second_sem):
-    first = pltpu.make_async_copy(first_ref, first_out, first_sem)
-    second = pltpu.make_async_copy(second_ref, second_out, second_sem)
+            out[which, :, here] = hold_ref[which, pl.ds(pl.multiple_of(first, group_rows), group_rows), :].astype(BF16)
+
+
+def mean_body(*refs):
+    shares, outs = refs[:-2], refs[-2:]
+    block = outs[0].shape[1]
+    here = pl.ds(pl.multiple_of(pl.program_id(0) * block, block), block)
+    for which, out in enumerate(outs):
+        total = shares[0][which, :, here].astype(F32)
+        for share in shares[1:]:
+            total += share[which, :, here].astype(F32)
+        out[...] = (total * (1.0 / len(shares))).astype(BF16)
+
+
+def land_body(first_col, span, first_ref, second_ref, *refs):
+    first_out, second_out, first_sem, second_sem = refs[-4:]
+    here = pl.ds(first_col, span)
+    first = pltpu.make_async_copy(first_ref, first_out.at[:, here], first_sem)
+    second = pltpu.make_async_copy(second_ref, second_out.at[:, here], second_sem)
     first.start()
     second.start()
     first.wait()
@@ -215,7 +230,7 @@
         scratch_shapes=[pltpu.VMEM((row_count, packed), F32), pltpu.VMEM((2, row_count, LANES), F32)],
         name="partials",
     )(fwd, saved, grad, norm_gain, down, up)
-    got = [near(parts[0])] + [near(send_step(parts[k], "tensor", k)) for k in range(1, share_count)]
+    got = [near(send_step(parts[k], "tensor", k)) for k in range(share_count - 1, 0, -1)] + [near(parts[0])]
     mine = pl.pallas_call(
         functools.partial(middle_body, unit_count, slot, full_width, seq_rows),
         in_specs=[smem] + [pl.BlockSpec(memory_space=pltpu.VMEM)] * share_count,
@@ -224,43 +239,61 @@
         name="middle",
     )(seq_lengths, *got)
     shares = [near(mine)] + [near(send_step(mine, "tensor", k)) for k in range(1, share_count)]
-    out_fwd, out_grad = pl.pallas_call(
-        functools.partial(edges_body, unit_count, slot, share_count, seq_rows),
-        grid=(steps,),
-        in_specs=[smem] + [whole] * share_count
-        + [cols(row_count), cols(row_count), cols(row_count), cols(1), cols(unit_count), cols(unit_count)],
-        out_specs=[whole] * 2,
-        out_shape=[pltpu.VMEM((row_count, width), BF16)] * 2,
-        scratch_shapes=[pltpu.VMEM((row_count, packed), BF16)],
-        name="edges",
-    )(seq_lengths, *shares, fwd, saved, grad, norm_gain, down, up)
-    next_grads = lax.ppermute(near(out_grad), "section", [(i + 1, i) for i in range(section_count - 1)])
-    next_inputs = lax.ppermute(near(out_fwd), "section", [(i, i + 1) for i in range(section_count - 1)])
+    span = width // CHUNKS
+    chunk_steps = span // block
+    landed = []
+    for c in range(CHUNKS):
+        part = lambda n, first=c * chunk_steps: pl.BlockSpec((n, block), lambda j: (0, j + first))
+        edge_rows = pl.pallas_call(
+            functools.partial(edges_body, unit_count, slot, share_count, seq_rows),
+            grid=(chunk_steps,),
+            in_specs=[smem] + [whole] * share_count
+            + [part(row_count), part(row_count), part(row_count), part(1), part(unit_count), part(unit_count)],
+            out_specs=[whole] * 2,
+            out_shape=[pltpu.VMEM((row_count, span), BF16)] * 2,
+            scratch_shapes=[pltpu.VMEM((row_count, packed), BF16)],
+            cost_estimate=pl.CostEstimate(flops=40 * row_count * unit_count * span, bytes_accessed=8 * row_count * span, transcendentals=0),
+            name="edges",
+        )
+        out_fwd, out_grad = edge_rows(seq_lengths, *shares, fwd, saved, grad, norm_gain, down, up)
+        next_grads = lax.ppermute(near(out_grad), "section", [(i + 1, i) for i in range(section_count - 1)])
+        next_inputs = lax.ppermute(near(out_fwd), "section", [(i, i + 1) for i in range(section_count - 1)])
+        landed.append((next_inputs, next_grads))
     group_rows = unit_count // group_count
     sum_maps = pl.pallas_call(
         functools.partial(grads_body, unit_count, slot, share_count),
         grid=(steps,),
         in_specs=[whole] * share_count + [cols(row_count), cols(row_count), cols(1)],
-        out_specs=[pl.BlockSpec((2, group_rows, block), lambda j: (0, 0, j))] * group_count,
-        out_shape=[jax.ShapeDtypeStruct((2, group_rows, width), BF16)] * group_count,
+        out_specs=[whole] * group_count,
+        out_shape=[pltpu.VMEM((2, group_rows, width), BF16)] * group_count,
         scratch_shapes=[pltpu.VMEM((row_count, packed), BF16), pltpu.VMEM((2, unit_count, block), F32)],
         cost_estimate=pl.CostEstimate(flops=40 * row_count * unit_count * width, bytes_accessed=6 * row_count * width, transcendentals=0),
         name="grads",
     )
     halves = sum_maps(*shares, saved, grad, norm_gain)
-    total = halves[0].astype(F32)
-    for k in range(1, group_count):
-        total += send_step(halves[k], "dp", k).astype(F32)
-    mean = (total * (1.0 / group_count)).astype(BF16)
-    next_inputs, next_grads = pl.pallas_call(
-        land_body,
-        in_specs=[whole] * 2,
-        out_specs=[pl.BlockSpec(memory_space=pl.ANY)] * 2,
-        out_shape=[jax.ShapeDtypeStruct((row_count, width), BF16)] * 2,
-        scratch_shapes=[pltpu.SemaphoreType.DMA] * 2,
-        name="land",
-    )(near(next_inputs), near(next_grads))
-    return (next_inputs[None, None], next_grads[None, None], mean[0:1], mean[1:2])
+    sums = [near(halves[0])] + [near(send_step(near(halves[k]), "dp", k)) for k in range(1, group_count)]
+    mean_maps = pl.pallas_call(
+        mean_body,
+        grid=(steps,),
+        in_specs=[whole] * group_count,
+        out_specs=[cols(group_rows)] * 2,
+        out_shape=[jax.ShapeDtypeStruct((group_rows, width), BF16)] * 2,
+        name="means",
+    )
+    grad_down, grad_up = mean_maps(*sums)
+    outs = []
+    for c, pair in enumerate(landed):
+        outs = pl.pallas_call(
+            functools.partial(land_body, c * span, span),
+            in_specs=[whole] * 2 + [pl.BlockSpec(memory_space=pl.ANY)] * len(outs),
+            out_specs=[pl.BlockSpec(memory_space=pl.ANY)] * 2,
+            out_shape=[jax.ShapeDtypeStruct((row_count, width), BF16)] * 2,
+            input_output_aliases={2: 0, 3: 1} if outs else {},
+            scratch_shapes=[pltpu.SemaphoreType.DMA] * 2,
+            name="land",
+        )(*map(near, pair), *outs)
+    next_inputs, next_grads = outs
+    return (next_inputs[None, None], next_grads[None, None], grad_down[None], grad_up[None])
 
 
 def solution(mesh):

time: 56.3 us -> 57 us (1.012)
  waiting for transfers between devices: 25.8 us -> 16.7 us
  starting transfers between devices: 12.9 us -> 19.6 us
  Pallas kernels: 14 us -> 18.9 us
  other arithmetic: 1.65 us -> 0 us
    ppermute x1 -> x2, waiting for transfers between devices: 13.5 us -> 2.58 us  [shards(): lax.ppermute(near(out_fwd), 'section', [(i, i + 1) for i in range(section...]
    ppermute x1 -> x2, starting transfers between devices: 3.48 us -> 8.81 us  [shards(): lax.ppermute(near(out_fwd), 'section', [(i, i + 1) for i in range(section...]
    pallas_call x2 -> x5, Pallas kernels: 4.78 us -> 9.85 us  [the longest x2 5.45 us: shards(): edge_rows(seq_lengths, *shares, fwd, saved, grad, norm_gain, down, up)]
    ppermute x1 -> x2, waiting for transfers between devices: 4.16 us -> 6.87 us  [shards(): lax.ppermute(near(out_grad), 'section', [(i + 1, i) for i in range(sectio...]
    convert_element_type x1 -> x0, other arithmetic: 1.65 us -> none  [shards(): mean = (total * (1.0 / group_count)).astype(BF16)]
    ppermute x1 -> x2, starting transfers between devices: 1.29 us -> 2.57 us  [shards(): lax.ppermute(near(out_grad), 'section', [(i + 1, i) for i in range(sectio...]
    slice x1 -> x0, local copies, waits for them, and re-layouts: 0.93 us -> none  [shards(): mean[1:2]]
    ppermute x7, waiting for transfers between devices: 8.09 us -> 7.27 us  [send_step(): lax.ppermute(cells, axis, [(i, partner(i, step, count)) for i in range(co...]
  transfers between devices with their start and end apart: 9 -> 11, of which waited for: 8 -> 9; matrix products, arithmetic and copies ran while one was open for 5% -> 0% of each run, Pallas kernels for 6% -> 15%
where the time goes in v3:
time: 57 us; the launch traced here: 56.6 us
  starting transfers between devices  19.6 us (34%)
  Pallas kernels  18.9 us (33%)
  waiting for transfers between devices  16.7 us (29%)
  local copies, waits for them, and re-layouts  0.74 us (1%)
  between operations  0.71 us (1%)
    ppermute x2, starting transfers between devices, shards(): lax.ppermute(near(out_fwd), 'section', [(i, i + 1) for i in range(section...  8.81 us
    ppermute x7, starting transfers between devices, send_step(): lax.ppermute(cells, axis, [(i, partner(i, step, count)) for i in range(co...  8.17 us
    ppermute x7, waiting for transfers between devices, send_step(): lax.ppermute(cells, axis, [(i, partner(i, step, count)) for i in range(co...  7.27 us
    ppermute x2, waiting for transfers between devices, shards(): lax.ppermute(near(out_grad), 'section', [(i + 1, i) for i in range(sectio...  6.87 us
    pallas_call x2, Pallas kernels, shards(): edge_rows(seq_lengths, *shares, fwd, saved, grad, norm_gain, down, up)  5.45 us
    pallas_call x1, Pallas kernels, shards(): halves = sum_maps(*shares, saved, grad, norm_gain)  4.09 us
    pallas_call x1, Pallas kernels, shards(): pl.pallas_call(functools.partial(partials_body, unit_count, slot, share_c...  3.96 us
    pallas_call x2, Pallas kernels, shards(): pl.pallas_call(functools.partial(land_body, c * span, span), in_specs=[wh...  2.9 us
  transfers between devices with their start and end apart: 11, of which 9 were waited for; matrix products, arithmetic and copies ran while one was open for 0% of the time, Pallas kernels for 15%

profile of v3, /device:TPU:0, one launch (start us, length us, event | category | flops | bytes accessed | tf_op | source)
XLA Modules:
  0.0 56.6 jit_solution(4691954855280715987)
XLA Ops:
  0.6 4.0 %partials.1 = (bf16[48,768]{1,0:T(8,128)(2,1)S(1)}, bf16[48,768]{1,0:T(8,128)(2,1)S(1)}, bf16[48,768]{1,0:T(8,128)(2,1)S(1)}, bf16[48,768]{1,0:T(8,128)(2,1)S(1)}) custom-call(bf16[192,2048]{1,0:T(8,128)(2,1)} %bitcast.12, bf16[192,2048]{1,0:T(8,128)(2,1)} %bitcast.15, bf16[192,2048]{1,0:T(8,128)(2,1)} %bitcast.19, bf16[1,2048]{1,0:T(2,128)(2,1)} %refs_6_.1, ...), custom_call_target="tpu_custom_call" | custom-call | tf_op jit(solution)/shard_map/partials/pallas_call | solution.py:224
  4.6 4.0 %collective-permute-start = (bf16[48,768]{1,0:T(8,128)(2,1)S(1)}, bf16[48,768]{1,0:T(8,128)(2,1)S(1)}, u32[]{:S(2)}, u32[]{:S(2)}) collective-permute-start(bf16[48,768]{1,0:T(8,128)(2,1)S(1)} %get-tuple-element.20), channel_id=1, source_target_pairs={{0,6},{2,4},{4,2},{6,0},{1,7},{3,5},{5,3},{7,1},{8,14},{10,12},{12... | collective-permute-start | bytes 221192 | tf_op jit(solution)/shard_map/ppermute | solution.py:36
  8.6 0.5 collective-permute-start.1
  9.1 0.1 collective-permute-start.2
  9.2 1.7 %collective-permute-done.refs_0_ = bf16[48,768]{1,0:T(8,128)(2,1)S(1)} collective-permute-done((bf16[48,768]{1,0:T(8,128)(2,1)S(1)}, bf16[48,768]{1,0:T(8,128)(2,1)S(1)}, u32[]{:S(2)}, u32[]{:S(2)}) %collective-permute-start) | collective-permute-done | bytes 73760 | tf_op jit(solution)/shard_map/ppermute | solution.py:36
  10.9 2.0 %collective-permute-done.1.refs_1_ = bf16[48,768]{1,0:T(8,128)(2,1)S(1)} collective-permute-done((bf16[48,768]{1,0:T(8,128)(2,1)S(1)}, bf16[48,768]{1,0:T(8,128)(2,1)S(1)}, u32[]{:S(2)}, u32[]{:S(2)}) %collective-permute-start.1) | collective-permute-done | bytes 73760 | tf_op jit(solution)/shard_map/ppermute | solution.py:36
  12.9 0.5 collective-permute-done.2.refs_2_
  13.4 1.0 %middle.1.refs_0_ = bf16[48,768]{1,0:T(8,128)(2,1)S(1)} custom-call(s32[2]{0:T(128)} %bitcast.29, bf16[48,768]{1,0:T(8,128)(2,1)S(1)} %collective-permute-done.refs_0_, bf16[48,768]{1,0:T(8,128)(2,1)S(1)} %collective-permute-done.1.refs_1_, bf16[48,768]{1,0:T(8,128)(2,1)S(1)} %collective-permute-done.2.refs_2_, bf16[48,768]{1,0:T(8,128)(2,1)S(1)} %get-tuple-element.23.refs_3_), custom_call_target="tpu_custom_call" | custom-call | tf_op jit(solution)/shard_map/middle/pallas_call | solution.py:234
  14.4 1.6 %collective-permute-start.5 = (bf16[48,768]{1,0:T(8,128)(2,1)S(1)}, bf16[48,768]{1,0:T(8,128)(2,1)S(1)}, u32[]{:S(2)}, u32[]{:S(2)}) collective-permute-start(bf16[48,768]{1,0:T(8,128)(2,1)S(1)} %middle.1.refs_0_), channel_id=1, source_target_pairs={{0,6},{2,4},{4,2},{6,0},{1,7},{3,5},{5,3},{7,1},{8,14},{10,12},{12... | collective-permute-start | bytes 221192 | tf_op jit(solution)/shard_map/ppermute | solution.py:36
  16.0 0.7 %collective-permute-start.4 = (bf16[48,768]{1,0:T(8,128)(2,1)S(1)}, bf16[48,768]{1,0:T(8,128)(2,1)S(1)}, u32[]{:S(2)}, u32[]{:S(2)}) collective-permute-start(bf16[48,768]{1,0:T(8,128)(2,1)S(1)} %middle.1.refs_0_), channel_id=1, source_target_pairs={{0,4},{2,6},{4,0},{6,2},{1,5},{3,7},{5,1},{7,3},{8,12},{10,14},{12... | collective-permute-start | bytes 221192 | tf_op jit(solution)/shard_map/ppermute | solution.py:36
  16.7 1.3 %collective-permute-start.3 = (bf16[48,768]{1,0:T(8,128)(2,1)S(1)}, bf16[48,768]{1,0:T(8,128)(2,1)S(1)}, u32[]{:S(2)}, u32[]{:S(2)}) collective-permute-start(bf16[48,768]{1,0:T(8,128)(2,1)S(1)} %middle.1.refs_0_), channel_id=1, source_target_pairs={{0,2},{2,0},{4,6},{6,4},{1,3},{3,1},{5,7},{7,5},{8,10},{10,8},{12,... | collective-permute-start | bytes 221192 | tf_op jit(solution)/shard_map/ppermute | solution.py:36
  18.0 2.0 %collective-permute-done.5.refs_3_ = bf16[48,768]{1,0:T(8,128)(2,1)S(1)} collective-permute-done((bf16[48,768]{1,0:T(8,128)(2,1)S(1)}, bf16[48,768]{1,0:T(8,128)(2,1)S(1)}, u32[]{:S(2)}, u32[]{:S(2)}) %collective-permute-start.5) | collective-permute-done | bytes 73760 | tf_op jit(solution)/shard_map/ppermute | solution.py:36
  19.9 0.8 %collective-permute-done.4.refs_2_ = bf16[48,768]{1,0:T(8,128)(2,1)S(1)} collective-permute-done((bf16[48,768]{1,0:T(8,128)(2,1)S(1)}, bf16[48,768]{1,0:T(8,128)(2,1)S(1)}, u32[]{:S(2)}, u32[]{:S(2)}) %collective-permute-start.4) | collective-permute-done | bytes 73760 | tf_op jit(solution)/shard_map/ppermute | solution.py:36
  20.7 0.3 collective-permute-done.3.refs_1_
  21.0 4.1 %grads.1 = (bf16[2,96,2048]{2,1,0:T(8,128)(2,1)S(1)}, bf16[2,96,2048]{2,1,0:T(8,128)(2,1)}) custom-call(bf16[48,768]{1,0:T(8,128)(2,1)S(1)} %middle.1.refs_0_, bf16[48,768]{1,0:T(8,128)(2,1)S(1)} %collective-permute-done.3.refs_1_, bf16[48,768]{1,0:T(8,128)(2,1)S(1)} %collective-permute-done.4.refs_2_, bf16[48,768]{1,0:T(8,128)(2,1)S(1)} %collective-permute-done.5.refs_3_, ...), custom_call_target="tpu_custom_call" | custom-call | flops 3019898880 | bytes 2359296 | tf_op jit(solution)/shard_map/grads/pallas_call | solution.py:273
  25.1 0.0 collective-permute-start.10
  25.1 2.8 %edges.3 = (bf16[192,1024]{1,0:T(8,128)(2,1)}, bf16[192,1024]{1,0:T(8,128)(2,1)}) custom-call(s32[2]{0:T(128)} %bitcast.30, bf16[48,768]{1,0:T(8,128)(2,1)S(1)} %middle.1.refs_0_, bf16[48,768]{1,0:T(8,128)(2,1)S(1)} %collective-permute-done.3.refs_1_, bf16[48,768]{1,0:T(8,128)(2,1)S(1)} %collective-permute-done.4.refs_2_, ...), custom_call_target="tpu_custom_call" | custom-call | flops 1509949440 | bytes 1572864 | tf_op jit(solution)/shard_map/edges/pallas_call | solution.py:258
  27.9 4.2 %collective-permute-start.8 = (bf16[192,1024]{1,0:T(8,128)(2,1)}, bf16[192,1024]{1,0:T(8,128)(2,1)}, u32[]{:S(2)}, u32[]{:S(2)}) collective-permute-start(bf16[192,1024]{1,0:T(8,128)(2,1)} %get-tuple-element.26), channel_id=1, source_target_pairs={{0,8},{8,16},{16,24},{1,9},{9,17},{17,25},{2,10},{10,18},{18,26},{... | collective-permute-start | bytes 1179656 | tf_op jit(solution)/shard_map/ppermute | solution.py:260
  32.1 1.3 %collective-permute-start.9 = (bf16[192,1024]{1,0:T(8,128)(2,1)}, bf16[192,1024]{1,0:T(8,128)(2,1)}, u32[]{:S(2)}, u32[]{:S(2)}) collective-permute-start(bf16[192,1024]{1,0:T(8,128)(2,1)} %get-tuple-element.27), channel_id=1, source_target_pairs={{8,0},{16,8},{24,16},{9,1},{17,9},{25,17},{10,2},{18,10},{26,18},{... | collective-permute-start | bytes 1179656 | tf_op jit(solution)/shard_map/ppermute | solution.py:259
  33.4 2.7 %edges.2 = (bf16[192,1024]{1,0:T(8,128)(2,1)}, bf16[192,1024]{1,0:T(8,128)(2,1)S(1)}) custom-call(s32[2]{0:T(128)} %bitcast.31, bf16[48,768]{1,0:T(8,128)(2,1)S(1)} %middle.1.refs_0_, bf16[48,768]{1,0:T(8,128)(2,1)S(1)} %collective-permute-done.3.refs_1_, bf16[48,768]{1,0:T(8,128)(2,1)S(1)} %collective-permute-done.4.refs_2_, ...), custom_call_target="tpu_custom_call" | custom-call | flops 1509949440 | bytes 1572864 | tf_op jit(solution)/shard_map/edges/pallas_call | solution.py:258
  36.1 0.0 copy-start
  36.1 0.7 %copy-done = bf16[192,1024]{1,0:T(8,128)(2,1)} copy-done((bf16[192,1024]{1,0:T(8,128)(2,1)}, bf16[192,1024]{1,0:T(8,128)(2,1)S(1)}, u32[]{:S(2)}) %copy-start) | copy-done | bytes 393240
  36.9 4.6 %collective-permute-start.6 = (bf16[192,1024]{1,0:T(8,128)(2,1)}, bf16[192,1024]{1,0:T(8,128)(2,1)S(1)}, u32[]{:S(2)}, u32[]{:S(2)}) collective-permute-start(bf16[192,1024]{1,0:T(8,128)(2,1)} %get-tuple-element.24), channel_id=1, source_target_pairs={{0,8},{8,16},{16,24},{1,9},{9,17},{17,25},{2,10},{10,18},{18,26},{... | collective-permute-start | bytes 1179656 | tf_op jit(solution)/shard_map/ppermute | solution.py:260
  41.4 1.3 %collective-permute-start.7 = (bf16[192,1024]{1,0:T(8,128)(2,1)}, bf16[192,1024]{1,0:T(8,128)(2,1)S(1)}, u32[]{:S(2)}, u32[]{:S(2)}) collective-permute-start(bf16[192,1024]{1,0:T(8,128)(2,1)} %copy-done), channel_id=1, source_target_pairs={{8,0},{16,8},{24,16},{9,1},{17,9},{25,17},{10,2},{18,10},{26,18},{... | collective-permute-start | bytes 1179656 | tf_op jit(solution)/shard_map/ppermute | solution.py:259
  42.7 0.0 collective-permute-done.8.first_ref
  42.8 2.8 %collective-permute-done.9.second_ref = bf16[192,1024]{1,0:T(8,128)(2,1)} collective-permute-done((bf16[192,1024]{1,0:T(8,128)(2,1)}, bf16[192,1024]{1,0:T(8,128)(2,1)}, u32[]{:S(2)}, u32[]{:S(2)}) %collective-permute-start.9) | collective-permute-done | bytes 393248 | tf_op jit(solution)/shard_map/ppermute | solution.py:259
  45.6 2.0 %land.2 = (bf16[192,2048]{1,0:T(8,128)(2,1)}, bf16[192,2048]{1,0:T(8,128)(2,1)}) custom-call(bf16[192,1024]{1,0:T(8,128)(2,1)} %collective-permute-done.8.first_ref, bf16[192,1024]{1,0:T(8,128)(2,1)} %collective-permute-done.9.second_ref), custom_call_target="tpu_custom_call" | custom-call | tf_op jit(solution)/shard_map/land/pallas_call | solution.py:286
  47.6 2.6 %collective-permute-done.6.first_ref = bf16[192,1024]{1,0:T(8,128)(2,1)S(1)} collective-permute-done((bf16[192,1024]{1,0:T(8,128)(2,1)}, bf16[192,1024]{1,0:T(8,128)(2,1)S(1)}, u32[]{:S(2)}, u32[]{:S(2)}) %collective-permute-start.6) | collective-permute-done | bytes 393248 | tf_op jit(solution)/shard_map/ppermute | solution.py:260
  50.2 4.0 %collective-permute-done.7.second_ref = bf16[192,1024]{1,0:T(8,128)(2,1)S(1)} collective-permute-done((bf16[192,1024]{1,0:T(8,128)(2,1)}, bf16[192,1024]{1,0:T(8,128)(2,1)S(1)}, u32[]{:S(2)}, u32[]{:S(2)}) %collective-permute-start.7) | collective-permute-done | bytes 393248 | tf_op jit(solution)/shard_map/ppermute | solution.py:259
  54.2 0.9 %land.3 = (bf16[192,2048]{1,0:T(8,128)(2,1)}, bf16[192,2048]{1,0:T(8,128)(2,1)}) custom-call(bf16[192,1024]{1,0:T(8,128)(2,1)S(1)} %collective-permute-done.6.first_ref, bf16[192,1024]{1,0:T(8,128)(2,1)S(1)} %collective-permute-done.7.second_ref, bf16[192,2048]{1,0:T(8,128)(2,1)} %get-tuple-element.28.refs_0_, ...), custom_call_target="tpu_custom_call", output_to_operand_aliasing={{0}: (2, {}), {1}: (3, {})} | custom-call | tf_op jit(solution)/shard_map/land/pallas_call | solution.py:286
  55.1 0.0 collective-permute-done.10.refs_1_
  55.1 1.5 %means.1 = (bf16[96,2048]{1,0:T(8,128)(2,1)}, bf16[96,2048]{1,0:T(8,128)(2,1)}) custom-call(bf16[2,96,2048]{2,1,0:T(8,128)(2,1)S(1)} %get-tuple-element.32.refs_0_, bf16[2,96,2048]{2,1,0:T(8,128)(2,1)S(1)} %collective-permute-done.10.refs_1_), custom_call_target="tpu_custom_call" | custom-call | tf_op jit(solution)/shard_map/means/pallas_call | solution.py:283
Async XLA Ops:
  4.6 6.3 %collective-permute-start = (bf16[48,768]{1,0:T(8,128)(2,1)S(1)}, bf16[48,768]{1,0:T(8,128)(2,1)S(1)}, u32[]{:S(2)}, u32[]{:S(2)}) collective-permute-start(bf16[48,768]{1,0:T(8,128)(2,1)S(1)} %get-tuple-element.20), channel_id=1, source_target_pairs={{0,6},{2,4},{4,2},{6,0},{1,7},{3,5},{5,3},{7,1},{8,14},{10,12},{12... | collective-permute-start | bytes 221192 | tf_op jit(solution)/shard_map/ppermute | solution.py:36
  8.6 4.4 %collective-permute-start.1 = (bf16[48,768]{1,0:T(8,128)(2,1)S(1)}, bf16[48,768]{1,0:T(8,128)(2,1)S(1)}, u32[]{:S(2)}, u32[]{:S(2)}) collective-permute-start(bf16[48,768]{1,0:T(8,128)(2,1)S(1)} %get-tuple-element.21), channel_id=1, source_target_pairs={{0,4},{2,6},{4,0},{6,2},{1,5},{3,7},{5,1},{7,3},{8,12},{10,14},{12... | collective-permute-start | bytes 221192 | tf_op jit(solution)/shard_map/ppermute | solution.py:36
  9.1 4.4 %collective-permute-start.2 = (bf16[48,768]{1,0:T(8,128)(2,1)S(1)}, bf16[48,768]{1,0:T(8,128)(2,1)S(1)}, u32[]{:S(2)}, u32[]{:S(2)}) collective-permute-start(bf16[48,768]{1,0:T(8,128)(2,1)S(1)} %get-tuple-element.22), channel_id=1, source_target_pairs={{0,2},{2,0},{4,6},{6,4},{1,3},{3,1},{5,7},{7,5},{8,10},{10,8},{12,... | collective-permute-start | bytes 221192 | tf_op jit(solution)/shard_map/ppermute | solution.py:36
  14.4 5.5 %collective-permute-start.5 = (bf16[48,768]{1,0:T(8,128)(2,1)S(1)}, bf16[48,768]{1,0:T(8,128)(2,1)S(1)}, u32[]{:S(2)}, u32[]{:S(2)}) collective-permute-start(bf16[48,768]{1,0:T(8,128)(2,1)S(1)} %middle.1.refs_0_), channel_id=1, source_target_pairs={{0,6},{2,4},{4,2},{6,0},{1,7},{3,5},{5,3},{7,1},{8,14},{10,12},{12... | collective-permute-start | bytes 221192 | tf_op jit(solution)/shard_map/ppermute | solution.py:36
  16.0 4.7 %collective-permute-start.4 = (bf16[48,768]{1,0:T(8,128)(2,1)S(1)}, bf16[48,768]{1,0:T(8,128)(2,1)S(1)}, u32[]{:S(2)}, u32[]{:S(2)}) collective-permute-start(bf16[48,768]{1,0:T(8,128)(2,1)S(1)} %middle.1.refs_0_), channel_id=1, source_target_pairs={{0,4},{2,6},{4,0},{6,2},{1,5},{3,7},{5,1},{7,3},{8,12},{10,14},{12... | collective-permute-start | bytes 221192 | tf_op jit(solution)/shard_map/ppermute | solution.py:36
  16.7 4.4 %collective-permute-start.3 = (bf16[48,768]{1,0:T(8,128)(2,1)S(1)}, bf16[48,768]{1,0:T(8,128)(2,1)S(1)}, u32[]{:S(2)}, u32[]{:S(2)}) collective-permute-start(bf16[48,768]{1,0:T(8,128)(2,1)S(1)} %middle.1.refs_0_), channel_id=1, source_target_pairs={{0,2},{2,0},{4,6},{6,4},{1,3},{3,1},{5,7},{7,5},{8,10},{10,8},{12,... | collective-permute-start | bytes 221192 | tf_op jit(solution)/shard_map/ppermute | solution.py:36
  25.1 30.0 %collective-permute-start.10 = (bf16[2,96,2048]{2,1,0:T(8,128)(2,1)}, bf16[2,96,2048]{2,1,0:T(8,128)(2,1)S(1)}, u32[]{:S(2)}, u32[]{:S(2)}) collective-permute-start(bf16[2,96,2048]{2,1,0:T(8,128)(2,1)} %get-tuple-element.33), channel_id=1, source_target_pairs={{0,1},{1,0},{2,3},{3,2},{4,5},{5,4},{6,7},{7,6},{8,9},{9,8},{10,11... | collective-permute-start | bytes 2359304 | tf_op jit(solution)/shard_map/ppermute | solution.py:36
  27.9 14.8 %collective-permute-start.8 = (bf16[192,1024]{1,0:T(8,128)(2,1)}, bf16[192,1024]{1,0:T(8,128)(2,1)}, u32[]{:S(2)}, u32[]{:S(2)}) collective-permute-start(bf16[192,1024]{1,0:T(8,128)(2,1)} %get-tuple-element.26), channel_id=1, source_target_pairs={{0,8},{8,16},{16,24},{1,9},{9,17},{17,25},{2,10},{10,18},{18,26},{... | collective-permute-start | bytes 1179656 | tf_op jit(solution)/shard_map/ppermute | solution.py:260
  32.1 13.4 %collective-permute-start.9 = (bf16[192,1024]{1,0:T(8,128)(2,1)}, bf16[192,1024]{1,0:T(8,128)(2,1)}, u32[]{:S(2)}, u32[]{:S(2)}) collective-permute-start(bf16[192,1024]{1,0:T(8,128)(2,1)} %get-tuple-element.27), channel_id=1, source_target_pairs={{8,0},{16,8},{24,16},{9,1},{17,9},{25,17},{10,2},{18,10},{26,18},{... | collective-permute-start | bytes 1179656 | tf_op jit(solution)/shard_map/ppermute | solution.py:259
  36.1 0.7 %copy-start = (bf16[192,1024]{1,0:T(8,128)(2,1)}, bf16[192,1024]{1,0:T(8,128)(2,1)S(1)}, u32[]{:S(2)}) copy-start(bf16[192,1024]{1,0:T(8,128)(2,1)S(1)} %get-tuple-element.25) | copy-start | bytes 1179652
  36.9 13.3 %collective-permute-start.6 = (bf16[192,1024]{1,0:T(8,128)(2,1)}, bf16[192,1024]{1,0:T(8,128)(2,1)S(1)}, u32[]{:S(2)}, u32[]{:S(2)}) collective-permute-start(bf16[192,1024]{1,0:T(8,128)(2,1)} %get-tuple-element.24), channel_id=1, source_target_pairs={{0,8},{8,16},{16,24},{1,9},{9,17},{17,25},{2,10},{10,18},{18,26},{... | collective-permute-start | bytes 1179656 | tf_op jit(solution)/shard_map/ppermute | solution.py:260
  41.4 12.8 %collective-permute-start.7 = (bf16[192,1024]{1,0:T(8,128)(2,1)}, bf16[192,1024]{1,0:T(8,128)(2,1)S(1)}, u32[]{:S(2)}, u32[]{:S(2)}) collective-permute-start(bf16[192,1024]{1,0:T(8,128)(2,1)} %copy-done), channel_id=1, source_target_pairs={{8,0},{16,8},{24,16},{9,1},{17,9},{25,17},{10,2},{18,10},{26,18},{... | collective-permute-start | bytes 1179656 | tf_op jit(solution)/shard_map/ppermute | solution.py:259

commit v4 on v3

--- a/solution.py
+++ b/solution.py
@@ -10,7 +10,8 @@
 EPSILON = 1e-05
 LANES = 128
 BLOCK = 512
-CHUNKS = 2
+CHUNKS = 1
+KERNEL_VMEM = 32 * 1024 * 1024
 F32 = jnp.float32
 BF16 = jnp.bfloat16
 
@@ -236,6 +237,7 @@
         in_specs=[smem] + [pl.BlockSpec(memory_space=pltpu.VMEM)] * share_count,
         out_specs=pl.BlockSpec(memory_space=pltpu.VMEM),
         out_shape=share_type,
+        compiler_params=pltpu.CompilerParams(vmem_limit_bytes=KERNEL_VMEM),
         name="middle",
     )(seq_lengths, *got)
     shares = [near(mine)] + [near(send_step(mine, "tensor", k)) for k in range(1, share_count)]
@@ -253,6 +255,7 @@
             out_shape=[pltpu.VMEM((row_count, span), BF16)] * 2,
             scratch_shapes=[pltpu.VMEM((row_count, packed), BF16)],
             cost_estimate=pl.CostEstimate(flops=40 * row_count * unit_count * span, bytes_accessed=8 * row_count * span, transcendentals=0),
+            compiler_params=pltpu.CompilerParams(vmem_limit_bytes=KERNEL_VMEM),
             name="edges",
         )
         out_fwd, out_grad = edge_rows(seq_lengths, *shares, fwd, saved, grad, norm_gain, down, up)
@@ -268,6 +271,7 @@
         out_shape=[pltpu.VMEM((2, group_rows, width), BF16)] * group_count,
         scratch_shapes=[pltpu.VMEM((row_count, packed), BF16), pltpu.VMEM((2, unit_count, block), F32)],
         cost_estimate=pl.CostEstimate(flops=40 * row_count * unit_count * width, bytes_accessed=6 * row_count * width, transcendentals=0),
+        compiler_params=pltpu.CompilerParams(vmem_limit_bytes=KERNEL_VMEM),
         name="grads",
     )
     halves = sum_maps(*shares, saved, grad, norm_gain)
@@ -278,6 +282,7 @@
         in_specs=[whole] * group_count,
         out_specs=[cols(group_rows)] * 2,
         out_shape=[jax.ShapeDtypeStruct((group_rows, width), BF16)] * 2,
+        compiler_params=pltpu.CompilerParams(vmem_limit_bytes=KERNEL_VMEM),
         name="means",
     )
     grad_down, grad_up = mean_maps(*sums)
@@ -290,6 +295,7 @@
             out_shape=[jax.ShapeDtypeStruct((row_count, width), BF16)] * 2,
             input_output_aliases={2: 0, 3: 1} if outs else {},
             scratch_shapes=[pltpu.SemaphoreType.DMA] * 2,
+            compiler_params=pltpu.CompilerParams(vmem_limit_bytes=KERNEL_VMEM),
             name="land",
         )(*map(near, pair), *outs)
     next_inputs, next_grads = outs

time: 57 us -> 51.9 us (0.911)
  waiting for transfers between devices: 16.7 us -> 26 us
  Pallas kernels: 18.9 us -> 11.2 us
  starting transfers between devices: 19.6 us -> 13.1 us
    ppermute x2 -> x1, waiting for transfers between devices: 2.58 us -> 14.5 us  [shards(): lax.ppermute(near(out_fwd), 'section', [(i, i + 1) for i in range(section...]
    ppermute x2 -> x1, starting transfers between devices: 8.81 us -> 3.52 us  [shards(): lax.ppermute(near(out_fwd), 'section', [(i, i + 1) for i in range(section...]
    pallas_call x2 -> x1, Pallas kernels: 5.45 us -> 2.02 us  [shards(): edge_rows(seq_lengths, *shares, fwd, saved, grad, norm_gain, down, up)]
    ppermute x2 -> x1, waiting for transfers between devices: 6.87 us -> 4.16 us  [shards(): lax.ppermute(near(out_grad), 'section', [(i + 1, i) for i in range(sectio...]
    pallas_call x1, Pallas kernels: 4.09 us -> 1.62 us  [shards(): halves = sum_maps(*shares, saved, grad, norm_gain)]
    pallas_call x2 -> x1, Pallas kernels: 2.9 us -> 1.15 us  [shards(): pl.pallas_call(functools.partial(land_body, c * span, span), in_specs=[wh...]
    ppermute x2 -> x1, starting transfers between devices: 2.57 us -> 1.29 us  [shards(): lax.ppermute(near(out_grad), 'section', [(i + 1, i) for i in range(sectio...]
  transfers between devices with their start and end apart: 11 -> 9, of which waited for: 9 -> 8; matrix products, arithmetic and copies ran while one was open for 0% -> 0% of each run, Pallas kernels for 15% -> 7%
where the time goes in v4:
time: 51.9 us; the launch traced here: 51.7 us
  waiting for transfers between devices  26 us (50%)
  starting transfers between devices  13.1 us (25%)
  Pallas kernels  11.2 us (22%)
  between operations  0.76 us (1%)
  local copies, waits for them, and re-layouts  0.69 us (1%)
    ppermute x1, waiting for transfers between devices, shards(): lax.ppermute(near(out_fwd), 'section', [(i, i + 1) for i in range(section...  14.5 us
    ppermute x7, starting transfers between devices, send_step(): lax.ppermute(cells, axis, [(i, partner(i, step, count)) for i in range(co...  8.28 us
    ppermute x7, waiting for transfers between devices, send_step(): lax.ppermute(cells, axis, [(i, partner(i, step, count)) for i in range(co...  7.26 us
    ppermute x1, waiting for transfers between devices, shards(): lax.ppermute(near(out_grad), 'section', [(i + 1, i) for i in range(sectio...  4.16 us
    pallas_call x1, Pallas kernels, shards(): pl.pallas_call(functools.partial(partials_body, unit_count, slot, share_c...  4.05 us
    ppermute x1, starting transfers between devices, shards(): lax.ppermute(near(out_fwd), 'section', [(i, i + 1) for i in range(section...  3.52 us
    pallas_call x1, Pallas kernels, shards(): edge_rows(seq_lengths, *shares, fwd, saved, grad, norm_gain, down, up)  2.02 us
    pallas_call x1, Pallas kernels, shards(): halves = sum_maps(*shares, saved, grad, norm_gain)  1.62 us
  transfers between devices with their start and end apart: 9, of which 8 were waited for; matrix products, arithmetic and copies ran while one was open for 0% of the time, Pallas kernels for 7%

profile of v4, /device:TPU:0, one launch (start us, length us, event | category | flops | bytes accessed | tf_op | source)
XLA Modules:
  0.0 51.7 jit_solution(11217916249763758328)
XLA Ops:
  0.6 0.0 copy-start.1
  0.6 0.0 copy-start.2
  0.7 4.0 %partials.1 = (bf16[48,768]{1,0:T(8,128)(2,1)S(1)}, bf16[48,768]{1,0:T(8,128)(2,1)S(1)}, bf16[48,768]{1,0:T(8,128)(2,1)S(1)}, bf16[48,768]{1,0:T(8,128)(2,1)S(1)}) custom-call(bf16[192,2048]{1,0:T(8,128)(2,1)} %bitcast.10, bf16[192,2048]{1,0:T(8,128)(2,1)} %bitcast.12, bf16[192,2048]{1,0:T(8,128)(2,1)} %bitcast.15, bf16[1,2048]{1,0:T(2,128)(2,1)} %refs_6_.1, ...), custom_call_target="tpu_custom_call" | custom-call | tf_op jit(solution)/shard_map/partials/pallas_call | solution.py:225
  4.7 4.0 %collective-permute-start = (bf16[48,768]{1,0:T(8,128)(2,1)S(1)}, bf16[48,768]{1,0:T(8,128)(2,1)S(1)}, u32[]{:S(2)}, u32[]{:S(2)}) collective-permute-start(bf16[48,768]{1,0:T(8,128)(2,1)S(1)} %get-tuple-element.16), channel_id=1, source_target_pairs={{0,6},{2,4},{4,2},{6,0},{1,7},{3,5},{5,3},{7,1},{8,14},{10,12},{12... | collective-permute-start | bytes 221192 | tf_op jit(solution)/shard_map/ppermute | solution.py:37
  8.7 0.5 collective-permute-start.1
  9.2 0.1 collective-permute-start.2
  9.4 1.7 %collective-permute-done.refs_0_ = bf16[48,768]{1,0:T(8,128)(2,1)S(1)} collective-permute-done((bf16[48,768]{1,0:T(8,128)(2,1)S(1)}, bf16[48,768]{1,0:T(8,128)(2,1)S(1)}, u32[]{:S(2)}, u32[]{:S(2)}) %collective-permute-start) | collective-permute-done | bytes 73760 | tf_op jit(solution)/shard_map/ppermute | solution.py:37
  11.1 2.0 %collective-permute-done.1.refs_1_ = bf16[48,768]{1,0:T(8,128)(2,1)S(1)} collective-permute-done((bf16[48,768]{1,0:T(8,128)(2,1)S(1)}, bf16[48,768]{1,0:T(8,128)(2,1)S(1)}, u32[]{:S(2)}, u32[]{:S(2)}) %collective-permute-start.1) | collective-permute-done | bytes 73760 | tf_op jit(solution)/shard_map/ppermute | solution.py:37
  13.1 0.5 collective-permute-done.2.refs_2_
  13.6 0.0 copy-start.6
  13.6 0.7 %copy-done.6 = s32[1,1,2]{2,1,0:T(1,128)S(1)} copy-done((s32[1,1,2]{2,1,0:T(1,128)S(1)}, s32[1,1,2]{2,1,0:T(1,128)}, u32[]{:S(2)}) %copy-start.6) | copy-done | bytes 32
  14.2 0.0 copy-start.5
  14.2 0.9 %middle.1.refs_0_ = bf16[48,768]{1,0:T(8,128)(2,1)S(1)} custom-call(s32[2]{0:T(128)S(1)} %bitcast.22, bf16[48,768]{1,0:T(8,128)(2,1)S(1)} %collective-permute-done.refs_0_, bf16[48,768]{1,0:T(8,128)(2,1)S(1)} %collective-permute-done.1.refs_1_, bf16[48,768]{1,0:T(8,128)(2,1)S(1)} %collective-permute-done.2.refs_2_, bf16[48,768]{1,0:T(8,128)(2,1)S(1)} %get-tuple-element.19.refs_3_), custom_call_target="tpu_custom_call" | custom-call | tf_op jit(solution)/shard_map/middle/pallas_call | solution.py:235
  15.1 0.0 copy-start
  15.1 0.0 copy-start.3
  15.1 0.0 copy-start.4
  15.1 1.6 %collective-permute-start.5 = (bf16[48,768]{1,0:T(8,128)(2,1)S(1)}, bf16[48,768]{1,0:T(8,128)(2,1)S(1)}, u32[]{:S(2)}, u32[]{:S(2)}) collective-permute-start(bf16[48,768]{1,0:T(8,128)(2,1)S(1)} %middle.1.refs_0_), channel_id=1, source_target_pairs={{0,6},{2,4},{4,2},{6,0},{1,7},{3,5},{5,3},{7,1},{8,14},{10,12},{12... | collective-permute-start | bytes 221192 | tf_op jit(solution)/shard_map/ppermute | solution.py:37
  16.7 0.7 %collective-permute-start.4 = (bf16[48,768]{1,0:T(8,128)(2,1)S(1)}, bf16[48,768]{1,0:T(8,128)(2,1)S(1)}, u32[]{:S(2)}, u32[]{:S(2)}) collective-permute-start(bf16[48,768]{1,0:T(8,128)(2,1)S(1)} %middle.1.refs_0_), channel_id=1, source_target_pairs={{0,4},{2,6},{4,0},{6,2},{1,5},{3,7},{5,1},{7,3},{8,12},{10,14},{12... | collective-permute-start | bytes 221192 | tf_op jit(solution)/shard_map/ppermute | solution.py:37
  17.4 1.3 %collective-permute-start.3 = (bf16[48,768]{1,0:T(8,128)(2,1)S(1)}, bf16[48,768]{1,0:T(8,128)(2,1)S(1)}, u32[]{:S(2)}, u32[]{:S(2)}) collective-permute-start(bf16[48,768]{1,0:T(8,128)(2,1)S(1)} %middle.1.refs_0_), channel_id=1, source_target_pairs={{0,2},{2,0},{4,6},{6,4},{1,3},{3,1},{5,7},{7,5},{8,10},{10,8},{12,... | collective-permute-start | bytes 221192 | tf_op jit(solution)/shard_map/ppermute | solution.py:37
  18.7 2.0 %collective-permute-done.5.refs_3_ = bf16[48,768]{1,0:T(8,128)(2,1)S(1)} collective-permute-done((bf16[48,768]{1,0:T(8,128)(2,1)S(1)}, bf16[48,768]{1,0:T(8,128)(2,1)S(1)}, u32[]{:S(2)}, u32[]{:S(2)}) %collective-permute-start.5) | collective-permute-done | bytes 73760 | tf_op jit(solution)/shard_map/ppermute | solution.py:37
  20.7 0.8 %collective-permute-done.4.refs_2_ = bf16[48,768]{1,0:T(8,128)(2,1)S(1)} collective-permute-done((bf16[48,768]{1,0:T(8,128)(2,1)S(1)}, bf16[48,768]{1,0:T(8,128)(2,1)S(1)}, u32[]{:S(2)}, u32[]{:S(2)}) %collective-permute-start.4) | collective-permute-done | bytes 73760 | tf_op jit(solution)/shard_map/ppermute | solution.py:37
  21.4 0.3 collective-permute-done.3.refs_1_
  21.8 0.0 copy-done.1
  21.8 0.0 copy-done.2
  21.8 0.0 copy-done.5
  21.8 1.6 %grads.1 = (bf16[2,96,2048]{2,1,0:T(8,128)(2,1)S(1)}, bf16[2,96,2048]{2,1,0:T(8,128)(2,1)S(1)}) custom-call(bf16[48,768]{1,0:T(8,128)(2,1)S(1)} %middle.1.refs_0_, bf16[48,768]{1,0:T(8,128)(2,1)S(1)} %collective-permute-done.3.refs_1_, bf16[48,768]{1,0:T(8,128)(2,1)S(1)} %collective-permute-done.4.refs_2_, ...), custom_call_target="tpu_custom_call" | custom-call | flops 3019898880 | bytes 2359296 | tf_op jit(solution)/shard_map/grads/pallas_call | solution.py:277
  23.4 0.1 collective-permute-start.8
  23.5 0.0 copy-done
  23.5 0.0 copy-done.3
  23.5 0.0 copy-done.4
  23.5 2.0 %edges.1 = (bf16[192,2048]{1,0:T(8,128)(2,1)S(1)}, bf16[192,2048]{1,0:T(8,128)(2,1)S(1)}) custom-call(s32[2]{0:T(128)S(1)} %bitcast.23, bf16[48,768]{1,0:T(8,128)(2,1)S(1)} %middle.1.refs_0_, bf16[48,768]{1,0:T(8,128)(2,1)S(1)} %collective-permute-done.3.refs_1_, bf16[48,768]{1,0:T(8,128)(2,1)S(1)} %collective-permute-done.4.refs_2_, ...), custom_call_target="tpu_custom_call" | custom-call | flops 3019898880 | bytes 3145728 | tf_op jit(solution)/shard_map/edges/pallas_call | solution.py:261
  25.5 3.5 %collective-permute-start.6 = (bf16[192,2048]{1,0:T(8,128)(2,1)S(1)}, bf16[192,2048]{1,0:T(8,128)(2,1)S(1)}, u32[]{:S(2)}, u32[]{:S(2)}) collective-permute-start(bf16[192,2048]{1,0:T(8,128)(2,1)S(1)} %get-tuple-element.20), channel_id=1, source_target_pairs={{0,8},{8,16},{16,24},{1,9},{9,17},{17,25},{2,10},{10,18},{18,26},{... | collective-permute-start | bytes 2359304 | tf_op jit(solution)/shard_map/ppermute | solution.py:263
  29.1 1.3 %collective-permute-start.7 = (bf16[192,2048]{1,0:T(8,128)(2,1)S(1)}, bf16[192,2048]{1,0:T(8,128)(2,1)S(1)}, u32[]{:S(2)}, u32[]{:S(2)}) collective-permute-start(bf16[192,2048]{1,0:T(8,128)(2,1)S(1)} %get-tuple-element.21), channel_id=1, source_target_pairs={{8,0},{16,8},{24,16},{9,1},{17,9},{25,17},{10,2},{18,10},{26,18},{... | collective-permute-start | bytes 2359304 | tf_op jit(solution)/shard_map/ppermute | solution.py:262
  30.4 0.0 collective-permute-done.8.refs_1_
  30.4 1.5 %means.1 = (bf16[96,2048]{1,0:T(8,128)(2,1)}, bf16[96,2048]{1,0:T(8,128)(2,1)}) custom-call(bf16[2,96,2048]{2,1,0:T(8,128)(2,1)S(1)} %get-tuple-element.24.refs_0_, bf16[2,96,2048]{2,1,0:T(8,128)(2,1)S(1)} %collective-permute-done.8.refs_1_), custom_call_target="tpu_custom_call" | custom-call | tf_op jit(solution)/shard_map/means/pallas_call | solution.py:288
  31.9 14.5 %collective-permute-done.6.first_ref = bf16[192,2048]{1,0:T(8,128)(2,1)S(1)} collective-permute-done((bf16[192,2048]{1,0:T(8,128)(2,1)S(1)}, bf16[192,2048]{1,0:T(8,128)(2,1)S(1)}, u32[]{:S(2)}, u32[]{:S(2)}) %collective-permute-start.6) | collective-permute-done | bytes 786464 | tf_op jit(solution)/shard_map/ppermute | solution.py:263
  46.4 4.2 %collective-permute-done.7.second_ref = bf16[192,2048]{1,0:T(8,128)(2,1)S(1)} collective-permute-done((bf16[192,2048]{1,0:T(8,128)(2,1)S(1)}, bf16[192,2048]{1,0:T(8,128)(2,1)S(1)}, u32[]{:S(2)}, u32[]{:S(2)}) %collective-permute-start.7) | collective-permute-done | bytes 786464 | tf_op jit(solution)/shard_map/ppermute | solution.py:262
  50.6 1.2 %land.1 = (bf16[192,2048]{1,0:T(8,128)(2,1)}, bf16[192,2048]{1,0:T(8,128)(2,1)}) custom-call(bf16[192,2048]{1,0:T(8,128)(2,1)S(1)} %collective-permute-done.6.first_ref, bf16[192,2048]{1,0:T(8,128)(2,1)S(1)} %collective-permute-done.7.second_ref), custom_call_target="tpu_custom_call" | custom-call | tf_op jit(solution)/shard_map/land/pallas_call | solution.py:291
Async XLA Ops:
  0.6 21.1 %copy-start.1 = (bf16[1,1,192,2048]{3,2,1,0:T(8,128)(2,1)S(1)}, bf16[1,1,192,2048]{3,2,1,0:T(8,128)(2,1)}, u32[]{:S(2)}) copy-start(bf16[1,1,192,2048]{3,2,1,0:T(8,128)(2,1)} %param.8) | copy-start | bytes 2359300
  0.6 21.1 %copy-start.2 = (bf16[1,1,192,2048]{3,2,1,0:T(8,128)(2,1)S(1)}, bf16[1,1,192,2048]{3,2,1,0:T(8,128)(2,1)}, u32[]{:S(2)}) copy-start(bf16[1,1,192,2048]{3,2,1,0:T(8,128)(2,1)} %param.9) | copy-start | bytes 2359300
  4.7 6.4 %collective-permute-start = (bf16[48,768]{1,0:T(8,128)(2,1)S(1)}, bf16[48,768]{1,0:T(8,128)(2,1)S(1)}, u32[]{:S(2)}, u32[]{:S(2)}) collective-permute-start(bf16[48,768]{1,0:T(8,128)(2,1)S(1)} %get-tuple-element.16), channel_id=1, source_target_pairs={{0,6},{2,4},{4,2},{6,0},{1,7},{3,5},{5,3},{7,1},{8,14},{10,12},{12... | collective-permute-start | bytes 221192 | tf_op jit(solution)/shard_map/ppermute | solution.py:37
  8.7 4.4 %collective-permute-start.1 = (bf16[48,768]{1,0:T(8,128)(2,1)S(1)}, bf16[48,768]{1,0:T(8,128)(2,1)S(1)}, u32[]{:S(2)}, u32[]{:S(2)}) collective-permute-start(bf16[48,768]{1,0:T(8,128)(2,1)S(1)} %get-tuple-element.17), channel_id=1, source_target_pairs={{0,4},{2,6},{4,0},{6,2},{1,5},{3,7},{5,1},{7,3},{8,12},{10,14},{12... | collective-permute-start | bytes 221192 | tf_op jit(solution)/shard_map/ppermute | solution.py:37
  9.2 4.4 %collective-permute-start.2 = (bf16[48,768]{1,0:T(8,128)(2,1)S(1)}, bf16[48,768]{1,0:T(8,128)(2,1)S(1)}, u32[]{:S(2)}, u32[]{:S(2)}) collective-permute-start(bf16[48,768]{1,0:T(8,128)(2,1)S(1)} %get-tuple-element.18), channel_id=1, source_target_pairs={{0,2},{2,0},{4,6},{6,4},{1,3},{3,1},{5,7},{7,5},{8,10},{10,8},{12,... | collective-permute-start | bytes 221192 | tf_op jit(solution)/shard_map/ppermute | solution.py:37
  13.6 0.7 %copy-start.6 = (s32[1,1,2]{2,1,0:T(1,128)S(1)}, s32[1,1,2]{2,1,0:T(1,128)}, u32[]{:S(2)}) copy-start(s32[1,1,2]{2,1,0:T(1,128)} %param.10) | copy-start | bytes 28
  14.2 7.5 %copy-start.5 = (bf16[1,2048]{1,0:T(2,128)(2,1)S(1)}, bf16[1,2048]{1,0:T(2,128)(2,1)}, u32[]{:S(2)}) copy-start(bf16[1,2048]{1,0:T(2,128)(2,1)} %refs_6_.1) | copy-start | bytes 12292
  15.1 8.4 %copy-start = (bf16[1,1,192,2048]{3,2,1,0:T(8,128)(2,1)S(1)}, bf16[1,1,192,2048]{3,2,1,0:T(8,128)(2,1)}, u32[]{:S(2)}) copy-start(bf16[1,1,192,2048]{3,2,1,0:T(8,128)(2,1)} %param.7) | copy-start | bytes 2359300
  15.1 8.4 %copy-start.3 = (bf16[1,192,2048]{2,1,0:T(8,128)(2,1)S(1)}, bf16[1,192,2048]{2,1,0:T(8,128)(2,1)}, u32[]{:S(2)}) copy-start(bf16[1,192,2048]{2,1,0:T(8,128)(2,1)} %param.12) | copy-start | bytes 2359300
  15.1 8.4 %copy-start.4 = (bf16[1,192,2048]{2,1,0:T(8,128)(2,1)S(1)}, bf16[1,192,2048]{2,1,0:T(8,128)(2,1)}, u32[]{:S(2)}) copy-start(bf16[1,192,2048]{2,1,0:T(8,128)(2,1)} %param.13) | copy-start | bytes 2359300
  15.1 5.5 %collective-permute-start.5 = (bf16[48,768]{1,0:T(8,128)(2,1)S(1)}, bf16[48,768]{1,0:T(8,128)(2,1)S(1)}, u32[]{:S(2)}, u32[]{:S(2)}) collective-permute-start(bf16[48,768]{1,0:T(8,128)(2,1)S(1)} %middle.1.refs_0_), channel_id=1, source_target_pairs={{0,6},{2,4},{4,2},{6,0},{1,7},{3,5},{5,3},{7,1},{8,14},{10,12},{12... | collective-permute-start | bytes 221192 | tf_op jit(solution)/shard_map/ppermute | solution.py:37
  16.7 4.7 %collective-permute-start.4 = (bf16[48,768]{1,0:T(8,128)(2,1)S(1)}, bf16[48,768]{1,0:T(8,128)(2,1)S(1)}, u32[]{:S(2)}, u32[]{:S(2)}) collective-permute-start(bf16[48,768]{1,0:T(8,128)(2,1)S(1)} %middle.1.refs_0_), channel_id=1, source_target_pairs={{0,4},{2,6},{4,0},{6,2},{1,5},{3,7},{5,1},{7,3},{8,12},{10,14},{12... | collective-permute-start | bytes 221192 | tf_op jit(solution)/shard_map/ppermute | solution.py:37
  17.4 4.4 %collective-permute-start.3 = (bf16[48,768]{1,0:T(8,128)(2,1)S(1)}, bf16[48,768]{1,0:T(8,128)(2,1)S(1)}, u32[]{:S(2)}, u32[]{:S(2)}) collective-permute-start(bf16[48,768]{1,0:T(8,128)(2,1)S(1)} %middle.1.refs_0_), channel_id=1, source_target_pairs={{0,2},{2,0},{4,6},{6,4},{1,3},{3,1},{5,7},{7,5},{8,10},{10,8},{12,... | collective-permute-start | bytes 221192 | tf_op jit(solution)/shard_map/ppermute | solution.py:37
  23.4 7.0 %collective-permute-start.8 = (bf16[2,96,2048]{2,1,0:T(8,128)(2,1)S(1)}, bf16[2,96,2048]{2,1,0:T(8,128)(2,1)S(1)}, u32[]{:S(2)}, u32[]{:S(2)}) collective-permute-start(bf16[2,96,2048]{2,1,0:T(8,128)(2,1)S(1)} %get-tuple-element.25), channel_id=1, source_target_pairs={{0,1},{1,0},{2,3},{3,2},{4,5},{5,4},{6,7},{7,6},{8,9},{9,8},{10,11... | collective-permute-start | bytes 2359304 | tf_op jit(solution)/shard_map/ppermute | solution.py:37
  25.5 20.9 %collective-permute-start.6 = (bf16[192,2048]{1,0:T(8,128)(2,1)S(1)}, bf16[192,2048]{1,0:T(8,128)(2,1)S(1)}, u32[]{:S(2)}, u32[]{:S(2)}) collective-permute-start(bf16[192,2048]{1,0:T(8,128)(2,1)S(1)} %get-tuple-element.20), channel_id=1, source_target_pairs={{0,8},{8,16},{16,24},{1,9},{9,17},{17,25},{2,10},{10,18},{18,26},{... | collective-permute-start | bytes 2359304 | tf_op jit(solution)/shard_map/ppermute | solution.py:263
  29.1 21.5 %collective-permute-start.7 = (bf16[192,2048]{1,0:T(8,128)(2,1)S(1)}, bf16[192,2048]{1,0:T(8,128)(2,1)S(1)}, u32[]{:S(2)}, u32[]{:S(2)}) collective-permute-start(bf16[192,2048]{1,0:T(8,128)(2,1)S(1)} %get-tuple-element.21), channel_id=1, source_target_pairs={{8,0},{16,8},{24,16},{9,1},{17,9},{25,17},{10,2},{18,10},{26,18},{... | collective-permute-start | bytes 2359304 | tf_op jit(solution)/shard_map/ppermute | solution.py:262
